TPU v7x, 128 devices: a whole 4x4x4 slice. The times are simulated.
128 devices in a mesh: xy: 8 (over z, core), gz: 4 (over y), ta: 4 (over x).
Axes of the slice: x: 4, y: 4, z: 4, core: 2. Of those that a mesh axis runs over, the one named last changes fastest.
Arguments:
- right_side: float32 [8, 4, 4, 128, 128], P('xy', 'gz', 'ta'), may hold values from -40 to 40
- link_blocks: float32 [8, 4, 4, 9, 2, 32, 32, 128], P('xy', 'gz', 'ta'), may hold values from -0.75 to 0.75
Outputs:
- solution: float32 [8, 4, 4, 128, 128], P('xy', 'gz', 'ta')
- residual: float32 [8, 4, 4, 128, 128], P('xy', 'gz', 'ta')
All inputs are finite; a program needn't handle non-finite values.
Results may differ from a plain program's by a relative error of at most 0.00018.
Values sent between devices are 32-bit elements; how exact they have to be, the bound alone decides.
A program may use at most 128 MiB of HBM per device.

v0:
```python
import functools

import jax
import jax.numpy as jnp
from jax import lax
from jax.sharding import Mesh
from jax.sharding import PartitionSpec as P

DOF = 32
RHS = 2
CX = 1
NY = 8
CZ = 2
CT = 8
ITERS = 2
XY_GZ_TA = ("xy_0", "xy_1", "gz", "ta")
XY = ("xy_0", "xy_1")


mass_shift = 4.0
epsilon = 1e-06


def extended(value, sides, width):
    edges = {}
    for axis, dim in sides:
        peers, length = (lax.axis_size(axis), value.shape[dim])
        up = [(i, (i + 1) % peers) for i in range(peers)]
        last = lax.slice_in_dim(value, length - width, length, axis=dim)
        initial = lax.slice_in_dim(value, 0, width, axis=dim)
        edges[dim] = (
            lax.ppermute(last, axis, up),
            lax.ppermute(initial, axis, [(b, a) for a, b in up]),
        )
    done = []
    for _, dim in sides:
        low, high = edges[dim]
        around = [(width, width) if d in done else (0, 0) for d in range(value.ndim)]
        value = jnp.concatenate([jnp.pad(low, around), value, jnp.pad(high, around)], axis=dim)
        done.append(dim)
    return value


def over_axes(value, axes):
    return functools.reduce(lax.psum, axes, value)


def split_parts(joined):
    shaped = joined.reshape(joined.shape[:-1] + (RHS, 2, DOF))
    return (shaped[..., 0, :], shaped[..., 1, :])


def join_parts(real, imaginary):
    stacked = jnp.stack((real, imaginary), -2)
    return stacked.reshape(stacked.shape[:-3] + (-1,))


def column_sums(values):
    folded = jnp.sum(values, axis=-1)
    return jnp.sum(folded.reshape(-1, folded.shape[-1]), axis=0)


def stacked_product(blocks, field):
    return jnp.einsum("...kcds,...ksrd->...src", blocks, field, precision=lax.Precision.HIGHEST)


def apply_operator(link_blocks, real, imaginary):
    joined = join_parts(real, imaginary)
    grid = joined.reshape(CX, NY, CZ, CT, joined.shape[-1])
    padded = extended(grid, ((XY, 0), ("gz", 2), ("ta", 3)), 1)
    nearby = [
        grid,
        padded[2:, :, 1:-1, 1:-1],
        padded[:-2, :, 1:-1, 1:-1],
        jnp.roll(grid, -1, 1),
        jnp.roll(grid, 1, 1),
        padded[1:-1, :, 2:, 1:-1],
        padded[1:-1, :, :-2, 1:-1],
        padded[1:-1, :, 1:-1, 2:],
        padded[1:-1, :, 1:-1, :-2],
    ]
    stacked = jnp.stack([piece.reshape(joined.shape) for piece in nearby], -3)
    near_real, near_imag = split_parts(stacked)
    blocks_real = link_blocks[..., 0, :, :, :]
    blocks_imag = link_blocks[..., 1, :, :, :]
    out_real = (
        mass_shift * real
        + stacked_product(blocks_real, near_real)
        - stacked_product(blocks_imag, near_imag)
    )
    output_imaginary = (
        mass_shift * imaginary
        + stacked_product(blocks_real, near_imag)
        + stacked_product(blocks_imag, near_real)
    )
    return (out_real, output_imaginary)


def project_out(basis, work_real, work_imag, proj_real, proj_imag):
    for index in range(len(basis)):
        coef_real = proj_real[index][:, None]
        coef_imag = proj_imag[index][:, None]
        vector = basis[index]
        work_real = work_real - (coef_real * vector[0] - coef_imag * vector[1])
        work_imag = work_imag - (coef_real * vector[1] + coef_imag * vector[0])
    return (work_real, work_imag)


def solve_positive_definite(matrix, target):
    size = matrix.shape[0]
    lower = {}
    for row in range(size):
        for col in range(row + 1):
            value = matrix[row, col]
            for inner in range(col):
                value = value - lower[row, inner] * lower[col, inner]
            if row == col:
                lower[row, row] = jnp.sqrt(value)
            else:
                lower[row, col] = value / lower[col, col]
    forward = []
    for row in range(size):
        value = target[row]
        for inner in range(row):
            value = value - lower[row, inner] * forward[inner]
        forward.append(value / lower[row, row])
    answer = [None] * size
    for row in reversed(range(size)):
        value = forward[row]
        for inner in range(row + 1, size):
            value = value - lower[inner, row] * answer[inner]
        answer[row] = value / lower[row, row]
    return jnp.stack(answer)


def least_squares(hessenberg_real, hessenberg_imaginary, beta):
    exact_answer_vector = lax.Precision.HIGHEST
    gram_matrix_real = jnp.einsum(
        "sxm,szm->xzm", hessenberg_real, hessenberg_real, precision=exact_answer_vector
    ) + jnp.einsum(
        "sxm,szm->xzm", hessenberg_imaginary, hessenberg_imaginary, precision=exact_answer_vector
    )
    gram_matrix_imaginary = jnp.einsum(
        "sxm,szm->xzm", hessenberg_real, hessenberg_imaginary, precision=exact_answer_vector
    ) - jnp.einsum(
        "sxm,szm->xzm", hessenberg_imaginary, hessenberg_real, precision=exact_answer_vector
    )
    upper = jnp.concatenate((gram_matrix_real, -gram_matrix_imaginary), 1)
    bottom = jnp.concatenate((gram_matrix_imaginary, gram_matrix_real), 1)
    system = jnp.concatenate((upper, bottom), 0)
    target = jnp.concatenate(
        (beta[None, :] * hessenberg_real[0], -beta[None, :] * hessenberg_imaginary[0]), 0
    )
    answer = solve_positive_definite(system, target)
    return (answer[:ITERS], answer[ITERS:])


def shards(right_side, link_blocks):
    rhs_real, rhs_imag = split_parts(right_side)
    start_sum = over_axes(column_sums(rhs_real * rhs_real + rhs_imag * rhs_imag), XY_GZ_TA)
    beta = jnp.sqrt(start_sum + epsilon)
    basis = [(rhs_real / beta[:, None], rhs_imag / beta[:, None])]
    hessenberg_real = jnp.zeros((ITERS + 1, ITERS, RHS), jnp.float32)
    hessenberg_imaginary = jnp.zeros((ITERS + 1, ITERS, RHS), jnp.float32)
    for step in range(ITERS):
        work_real, work_imag = apply_operator(link_blocks, basis[step][0], basis[step][1])
        proj_real = jnp.stack(
            [column_sums(vector[0] * work_real + vector[1] * work_imag) for vector in basis]
        )
        proj_imag = jnp.stack(
            [column_sums(vector[0] * work_imag - vector[1] * work_real) for vector in basis]
        )
        own_squares = column_sums(work_real * work_real + work_imag * work_imag)
        proj_real, proj_imag, squares = (
            over_axes(proj_real, XY_GZ_TA),
            over_axes(proj_imag, XY_GZ_TA),
            over_axes(own_squares, XY_GZ_TA),
        )
        work_real, work_imag = project_out(basis, work_real, work_imag, proj_real, proj_imag)
        leftover = squares - jnp.sum(proj_real * proj_real + proj_imag * proj_imag, axis=0)
        norm = jnp.sqrt(leftover + epsilon)
        hessenberg_real = hessenberg_real.at[: step + 1, step].set(proj_real)
        hessenberg_imaginary = hessenberg_imaginary.at[: step + 1, step].set(proj_imag)
        hessenberg_real = hessenberg_real.at[step + 1, step].set(norm)
        basis.append((work_real / norm[:, None], work_imag / norm[:, None]))
    coef_real, coef_imag = least_squares(hessenberg_real, hessenberg_imaginary, beta)
    sol_real = jnp.zeros_like(rhs_real)
    sol_imag = jnp.zeros_like(rhs_imag)
    for index in range(ITERS):
        weight_real = coef_real[index][:, None]
        weight_imag = coef_imag[index][:, None]
        sol_real = sol_real + weight_real * basis[index][0] - weight_imag * basis[index][1]
        sol_imag = sol_imag + weight_real * basis[index][1] + weight_imag * basis[index][0]
    exact_answer_vector = lax.Precision.HIGHEST
    mixed_real = jnp.einsum(
        "ijr,jr->ir", hessenberg_real, coef_real, precision=exact_answer_vector
    ) - jnp.einsum("ijr,jr->ir", hessenberg_imaginary, coef_imag, precision=exact_answer_vector)
    mixed_imag = jnp.einsum(
        "ijr,jr->ir", hessenberg_real, coef_imag, precision=exact_answer_vector
    ) + jnp.einsum("ijr,jr->ir", hessenberg_imaginary, coef_real, precision=exact_answer_vector)
    image_real = jnp.zeros_like(rhs_real)
    image_imag = jnp.zeros_like(rhs_imag)
    for index in range(ITERS + 1):
        weight_real = mixed_real[index][:, None]
        weight_imag = mixed_imag[index][:, None]
        image_real = image_real + weight_real * basis[index][0] - weight_imag * basis[index][1]
        image_imag = image_imag + weight_real * basis[index][1] + weight_imag * basis[index][0]
    return (
        join_parts(sol_real, sol_imag),
        join_parts(rhs_real - image_real, rhs_imag - image_imag),
    )


def solution(mesh):
    finer = Mesh(
        mesh.devices.reshape(4, 2, mesh.shape["gz"], mesh.shape["ta"]), ("xy_0", "xy_1", "gz", "ta")
    )
    return jax.shard_map(
        shards,
        mesh=finer,
        in_specs=(P(XY, "gz", "ta", None, None), P(XY, "gz", "ta", None, None, None, None, None)),
        out_specs=(P(XY, "gz", "ta", None, None), P(XY, "gz", "ta", None, None)),
        check_vma=False,
    )
```

profile of v0, /device:TPU:2, one launch (start us, length us, event | category | flops | bytes accessed | tf_op | source)
XLA Modules:
  0.0 328.9 jit_solution(17696563438914127399)
XLA Ops:
  1.7 11.7 %psum.196 = f32[2]{0:T(128)S(1)} all-reduce(f32[2]{0:T(128)S(1)} %fusion.49), channel_id=1, replica_groups=mesh['xy_0'=4,'xy_1'=2,'gz'=4,'ta'=4] {'xy_0'}, use_global_device_ids=true, to_apply=%region_1.0 | all-reduce | flops 2 | bytes 16 | tf_op jit(solution)/shard_map/psum | solution.py:45
  15.9 10.7 %psum.198 = f32[2]{0:T(128)S(1)} all-reduce(f32[2]{0:T(128)S(1)} %psum.197), channel_id=1, replica_groups=mesh['xy_0'=4,'xy_1'=2,'gz'=4,'ta'=4] {'gz'}, use_global_device_ids=true, to_apply=%region_3.0 | all-reduce | flops 2 | bytes 16 | tf_op jit(solution)/shard_map/psum | solution.py:45
  26.6 8.6 %psum.199 = f32[2]{0:T(128)S(1)} all-reduce(f32[2]{0:T(128)S(1)} %psum.198), channel_id=1, replica_groups=mesh['xy_0'=4,'xy_1'=2,'gz'=4,'ta'=4] {'ta'}, use_global_device_ids=true, to_apply=%region_4.0 | all-reduce | flops 2 | bytes 16 | tf_op jit(solution)/shard_map/psum | solution.py:45
  35.7 2.9 collective-permute-start
  40.7 2.5 collective-permute-start.4
  43.2 8.9 %fusion.68 = (f32[1,1,1,9,1,32,32,128]{7,6,5,4,3,2,1,0:T(8,128)}, f32[1,1,1,9,1,32,32,128]{7,6,5,4,3,2,1,0:T(8,128)}) fusion(f32[1,1,1,9,2,32,32,128]{7,6,5,4,3,2,1,0:T(8,128)} %param.15), kind=kLoop, calls=%fused_computation.204 | loop fusion | bytes 18874368 | tf_op jit(solution)/shard_map/slice | solution.py:84
  53.4 15.9 %copy.256 = f32[1,1,1,9,1,32,32,128]{6,5,3,7,4,2,1,0:T(8,128)} copy(f32[1,1,1,9,1,32,32,128]{7,6,5,4,3,2,1,0:T(8,128)} %get-tuple-element.154) | data formatting | bytes 9437184
  69.4 16.0 %copy.257 = f32[1,1,1,9,1,32,32,128]{6,5,3,7,4,2,1,0:T(8,128)} copy(f32[1,1,1,9,1,32,32,128]{7,6,5,4,3,2,1,0:T(8,128)} %get-tuple-element.155) | data formatting | bytes 9437184
  85.4 3.5 %collective-permute-done.5 = f32[1,8,2,1,128]{4,3,2,1,0:T(1,128)S(1)} collective-permute-done((f32[1,8,2,1,128]{4,3,2,1,0:T(1,128)S(1)}, f32[1,8,2,1,128]{4,3,2,1,0:T(1,128)S(1)}, u32[]{:S(2)}, u32[]{:S(2)}) %collective-permute-start.5) | collective-permute-done | bytes 8224 | tf_op jit(solution)/shard_map/ppermute | solution.py:32
  94.1 20.3 %fusion.16 = f32[128,2,32]{2,1,0:T(2,128)S(1)} fusion(f32[9,128,2,32]{3,2,0,1:T(2,128)S(1)} %copy.168, f32[1,1,1,9,1,32,32,128]{6,5,3,7,4,2,1,0:T(8,128)} %copy.256), kind=kOutput, calls=%fused_computation.16 | convolution fusion | flops 28311552 | bytes 5046272 | tf_op jit(solution)/shard_map/...kcds,...ksrd->...src/dot_general | solution.py:64
  114.5 17.2 %fusion.19 = f32[128,2,32]{2,1,0:T(2,128)S(1)} fusion(f32[9,128,2,32]{3,2,0,1:T(2,128)S(1)} %copy.171, f32[1,1,1,9,1,32,32,128]{6,5,3,7,4,2,1,0:T(8,128)S(1)} %copy-done), kind=kOutput, calls=%fused_computation.17 | convolution fusion | flops 28311552 | bytes 5046272 | tf_op jit(solution)/shard_map/...kcds,...ksrd->...src/dot_general | solution.py:64
  131.6 19.6 %fusion.28 = f32[128,2,32]{2,1,0:T(2,128)S(1)} fusion(f32[9,128,2,32]{3,2,0,1:T(2,128)S(1)} %copy.171, f32[1,1,1,9,1,32,32,128]{6,5,3,7,4,2,1,0:T(8,128)} %copy.257), kind=kOutput, calls=%fused_computation.20 | convolution fusion | flops 28311552 | bytes 5046272 | tf_op jit(solution)/shard_map/...kcds,...ksrd->...src/dot_general | solution.py:64
  151.2 17.7 %fusion.31 = f32[128,2,32]{2,1,0:T(2,128)S(1)} fusion(f32[9,128,2,32]{3,2,0,1:T(2,128)S(1)} %copy.168, f32[1,1,1,9,1,32,32,128]{6,5,3,7,4,2,1,0:T(8,128)S(1)} %bitcast.515), kind=kOutput, calls=%fused_computation.21 | convolution fusion | flops 28311552 | bytes 5046272 | tf_op jit(solution)/shard_map/...kcds,...ksrd->...src/dot_general | solution.py:64
  169.5 7.7 %all-reduce.15 = (f32[2]{0:T(128)S(1)}, f32[1,2]{1,0:T(1,128)S(1)}, f32[1,2]{1,0:T(1,128)S(1)}) all-reduce(f32[2]{0:T(128)S(1)} %get-tuple-element.92, f32[1,2]{1,0:T(1,128)S(1)} %bitcast.545, f32[1,2]{1,0:T(1,128)S(1)} %bitcast.544), channel_id=1, replica_groups=mesh['xy_0'=4,'xy_1'=2,'gz'=4,'ta'=4] {'xy_0'}, use_global_device_ids=true, to_apply=%region_11.12 | all-reduce | flops 6 | bytes 48 | tf_op jit(solution)/shard_map/psum | solution.py:45
  179.7 9.0 %all-reduce.13 = (f32[2]{0:T(128)S(1)}, f32[1,2]{1,0:T(1,128)S(1)}, f32[1,2]{1,0:T(1,128)S(1)}) all-reduce(f32[2]{0:T(128)S(1)} %get-tuple-element.127, f32[1,2]{1,0:T(1,128)S(1)} %get-tuple-element.128, f32[1,2]{1,0:T(1,128)S(1)} %get-tuple-element.129), channel_id=1, replica_groups=mesh['xy_0'=4,'xy_1'=2,'gz'=4,'ta'=4] {'gz'}, use_global_device_ids=true, to_apply=%region_13.14 | all-reduce | flops 6 | bytes 48 | tf_op jit(solution)/shard_map/psum | solution.py:45
  188.7 9.0 %all-reduce.11 = (f32[2]{0:T(128)S(1)}, f32[1,2]{1,0:T(1,128)S(1)}, f32[1,2]{1,0:T(1,128)S(1)}) all-reduce(f32[2]{0:T(128)S(1)} %get-tuple-element.115, f32[1,2]{1,0:T(1,128)S(1)} %get-tuple-element.116, f32[1,2]{1,0:T(1,128)S(1)} %get-tuple-element.117), channel_id=1, replica_groups=mesh['xy_0'=4,'xy_1'=2,'gz'=4,'ta'=4] {'ta'}, use_global_device_ids=true, to_apply=%region_14.15 | all-reduce | flops 6 | bytes 48 | tf_op jit(solution)/shard_map/psum | solution.py:45
  198.2 2.9 collective-permute-start.6
  212.6 19.4 %fusion.37 = f32[128,2,32]{2,1,0:T(2,128)S(1)} fusion(f32[9,128,2,32]{3,2,0,1:T(2,128)S(1)} %copy.218, f32[1,1,1,9,1,32,32,128]{6,5,3,7,4,2,1,0:T(8,128)} %copy.257), kind=kOutput, calls=%fused_computation.23 | convolution fusion | flops 28311552 | bytes 5046272 | tf_op jit(solution)/shard_map/...kcds,...ksrd->...src/dot_general | solution.py:64
  232.0 19.4 %fusion.22 = f32[128,2,32]{2,1,0:T(2,128)S(1)} fusion(f32[9,128,2,32]{3,2,0,1:T(2,128)S(1)} %copy.218, f32[1,1,1,9,1,32,32,128]{6,5,3,7,4,2,1,0:T(8,128)} %copy.256), kind=kOutput, calls=%fused_computation.18 | convolution fusion | flops 28311552 | bytes 5046272 | tf_op jit(solution)/shard_map/...kcds,...ksrd->...src/dot_general | solution.py:64
  252.6 19.4 %fusion.25 = f32[128,2,32]{2,1,0:T(2,128)S(1)} fusion(f32[9,128,2,32]{3,2,0,1:T(2,128)S(1)} %copy.221, f32[1,1,1,9,1,32,32,128]{6,5,3,7,4,2,1,0:T(8,128)} %copy.256), kind=kOutput, calls=%fused_computation.19 | convolution fusion | flops 28311552 | bytes 5046272 | tf_op jit(solution)/shard_map/...kcds,...ksrd->...src/dot_general | solution.py:64
  272.0 19.6 %fusion.34 = f32[128,2,32]{2,1,0:T(2,128)S(1)} fusion(f32[9,128,2,32]{3,2,0,1:T(2,128)S(1)} %copy.221, f32[1,1,1,9,1,32,32,128]{6,5,3,7,4,2,1,0:T(8,128)} %copy.257), kind=kOutput, calls=%fused_computation.22 | convolution fusion | flops 28311552 | bytes 5046272 | tf_op jit(solution)/shard_map/...kcds,...ksrd->...src/dot_general | solution.py:64
  292.2 8.5 %all-reduce.14 = (f32[2,2]{1,0:T(2,128)S(1)}, f32[2,2]{1,0:T(2,128)S(1)}, f32[2]{0:T(128)S(1)}) all-reduce(f32[2,2]{1,0:T(2,128)S(1)} %pad_maximum_fusion.21, f32[2,2]{1,0:T(2,128)S(1)} %pad_maximum_fusion.20, f32[2]{0:T(128)S(1)} %get-tuple-element.89), channel_id=1, replica_groups=mesh['xy_0'=4,'xy_1'=2,'gz'=4,'ta'=4] {'xy_0'}, use_global_device_ids=true, to_apply=%region_33.34 | all-reduce | flops 10 | bytes 80 | tf_op jit(solution)/shard_map/psum | solution.py:45
  303.2 9.6 %all-reduce.12 = (f32[2,2]{1,0:T(2,128)S(1)}, f32[2,2]{1,0:T(2,128)S(1)}, f32[2]{0:T(128)S(1)}) all-reduce(f32[2,2]{1,0:T(2,128)S(1)} %get-tuple-element.124, f32[2,2]{1,0:T(2,128)S(1)} %get-tuple-element.125, f32[2]{0:T(128)S(1)} %get-tuple-element.126), channel_id=1, replica_groups=mesh['xy_0'=4,'xy_1'=2,'gz'=4,'ta'=4] {'gz'}, use_global_device_ids=true, to_apply=%region_35.36 | all-reduce | flops 10 | bytes 80 | tf_op jit(solution)/shard_map/psum | solution.py:45
  312.8 9.9 %all-reduce.10 = (f32[2,2]{1,0:T(2,128)S(1)}, f32[2,2]{1,0:T(2,128)S(1)}, f32[2]{0:T(128)S(1)}) all-reduce(f32[2,2]{1,0:T(2,128)S(1)} %get-tuple-element.112, f32[2,2]{1,0:T(2,128)S(1)} %get-tuple-element.113, f32[2]{0:T(128)S(1)} %get-tuple-element.114), channel_id=1, replica_groups=mesh['xy_0'=4,'xy_1'=2,'gz'=4,'ta'=4] {'ta'}, use_global_device_ids=true, to_apply=%region_36.37 | all-reduce | flops 10 | bytes 80 | tf_op jit(solution)/shard_map/psum | solution.py:45
  (178 shorter events, 37.1 us)
Async XLA Ops:
  35.7 49.7 %collective-permute-start.1 = (f32[1,8,2,8,128]{4,3,2,1,0:T(8,128)S(1)}, f32[1,8,2,8,128]{4,3,2,1,0:T(8,128)S(1)}, u32[]{:S(2)}, u32[]{:S(2)}) collective-permute-start(f32[1,8,2,8,128]{4,3,2,1,0:T(8,128)S(1)} %reshape_reshape.6), channel_id=1, source_target_pairs={{0,16},{16,32},{32,48},{48,64},{64,80},{80,96},{96,112},{112,0},{1... | collective-permute-start | bytes 196616 | tf_op jit(solution)/shard_map/ppermute | solution.py:32
  35.7 49.7 %collective-permute-start = (f32[1,8,2,8,128]{4,3,2,1,0:T(8,128)S(1)}, f32[1,8,2,8,128]{4,3,2,1,0:T(8,128)S(1)}, u32[]{:S(2)}, u32[]{:S(2)}) collective-permute-start(f32[1,8,2,8,128]{4,3,2,1,0:T(8,128)S(1)} %reshape_reshape.6), channel_id=1, source_target_pairs={{16,0},{32,16},{48,32},{64,48},{80,64},{96,80},{112,96},{0,112},{1... | collective-permute-start | bytes 196616 | tf_op jit(solution)/shard_map/ppermute | solution.py:33
  38.7 46.6 %collective-permute-start.2 = (f32[1,8,1,8,128]{4,3,2,1,0:T(8,128)S(1)}, f32[1,8,1,8,128]{4,3,2,1,0:T(8,128)S(1)}, u32[]{:S(2)}, u32[]{:S(2)}) collective-permute-start(f32[1,8,1,8,128]{4,3,2,1,0:T(8,128)S(1)} %get-tuple-element.185), channel_id=1, source_target_pairs={{4,0},{8,4},{12,8},{0,12},{5,1},{9,5},{13,9},{1,13},{6,2},{10,6},{... | collective-permute-start | bytes 98312 | tf_op jit(solution)/shard_map/ppermute | solution.py:33
  38.7 46.7 %collective-permute-start.3 = (f32[1,8,1,8,128]{4,3,2,1,0:T(8,128)S(1)}, f32[1,8,1,8,128]{4,3,2,1,0:T(8,128)S(1)}, u32[]{:S(2)}, u32[]{:S(2)}) collective-permute-start(f32[1,8,1,8,128]{4,3,2,1,0:T(8,128)S(1)} %get-tuple-element.184), channel_id=1, source_target_pairs={{0,4},{4,8},{8,12},{12,0},{1,5},{5,9},{9,13},{13,1},{2,6},{6,10},{... | collective-permute-start | bytes 98312 | tf_op jit(solution)/shard_map/ppermute | solution.py:32
  40.7 44.7 %collective-permute-start.4 = (f32[1,8,2,1,128]{4,3,2,1,0:T(1,128)S(1)}, f32[1,8,2,1,128]{4,3,2,1,0:T(1,128)S(1)}, u32[]{:S(2)}, u32[]{:S(2)}) collective-permute-start(f32[1,8,2,1,128]{4,3,2,1,0:T(1,128)S(1)} %get-tuple-element.183), channel_id=1, source_target_pairs={{1,0},{2,1},{3,2},{0,3},{5,4},{6,5},{7,6},{4,7},{9,8},{10,9},{11,1... | collective-permute-start | bytes 24584 | tf_op jit(solution)/shard_map/ppermute | solution.py:33
  85.3 3.7 %collective-permute-start.5 = (f32[1,8,2,1,128]{4,3,2,1,0:T(1,128)S(1)}, f32[1,8,2,1,128]{4,3,2,1,0:T(1,128)S(1)}, u32[]{:S(2)}, u32[]{:S(2)}) collective-permute-start(f32[1,8,2,1,128]{4,3,2,1,0:T(1,128)S(1)} %get-tuple-element.182), channel_id=1, source_target_pairs={{0,1},{1,2},{2,3},{3,0},{4,5},{5,6},{6,7},{7,4},{8,9},{9,10},{10,1... | collective-permute-start | bytes 24584 | tf_op jit(solution)/shard_map/ppermute | solution.py:32
  94.1 20.4 %copy-start = (f32[1,1,1,9,1,32,32,128]{6,5,3,7,4,2,1,0:T(8,128)S(1)}, f32[1,1,1,9,1,32,32,128]{6,5,3,7,4,2,1,0:T(8,128)}, u32[]{:S(2)}) copy-start(f32[1,1,1,9,1,32,32,128]{6,5,3,7,4,2,1,0:T(8,128)} %copy.256) | copy-start | bytes 14155780
  114.4 36.8 %slice-start = ((s8[18874368]{0:T(1024)(128)(4,1)}), s8[2097152]{0:T(1024)(128)(4,1)S(1)}, s32[]{:S(2)}) async-start(s8[18874368]{0:T(1024)(128)(4,1)} %bitcast.514), calls=%async_computation | async-start | bytes 4194304
  114.4 36.8 %slice-start.1 = ((s8[18874368]{0:T(1024)(128)(4,1)}), s8[4194304]{0:T(1024)(128)(4,1)S(1)}, s32[]{:S(2)}) async-start(s8[18874368]{0:T(1024)(128)(4,1)} %bitcast.514), calls=%async_computation.1 | async-start | bytes 8388608
  114.5 36.7 %slice-start.2 = ((s8[18874368]{0:T(1024)(128)(4,1)}), s8[4194304]{0:T(1024)(128)(4,1)S(1)}, s32[]{:S(2)}) async-start(s8[18874368]{0:T(1024)(128)(4,1)} %bitcast.514), calls=%async_computation.2 | async-start | bytes 8388608
  131.6 19.6 %slice-start.3 = ((s8[18874368]{0:T(1024)(128)(4,1)}), s8[4194304]{0:T(1024)(128)(4,1)S(1)}, s32[]{:S(2)}) async-start(s8[18874368]{0:T(1024)(128)(4,1)} %bitcast.514), calls=%async_computation.3 | async-start | bytes 8388608
  131.6 19.6 %slice-start.4 = ((s8[18874368]{0:T(1024)(128)(4,1)}), s8[4194304]{0:T(1024)(128)(4,1)S(1)}, s32[]{:S(2)}) async-start(s8[18874368]{0:T(1024)(128)(4,1)} %bitcast.514), calls=%async_computation.4 | async-start | bytes 8388608
  198.2 9.0 %collective-permute-start.7 = (f32[1,8,2,8,128]{4,3,2,1,0:T(8,128)S(1)}, f32[1,8,2,8,128]{4,3,2,1,0:T(8,128)S(1)}, u32[]{:S(2)}, u32[]{:S(2)}) collective-permute-start(f32[1,8,2,8,128]{4,3,2,1,0:T(8,128)S(1)} %reshape_reshape.7), channel_id=1, source_target_pairs={{0,16},{16,32},{32,48},{48,64},{64,80},{80,96},{96,112},{112,0},{1... | collective-permute-start | bytes 196616 | tf_op jit(solution)/shard_map/ppermute | solution.py:32
  198.2 9.0 %collective-permute-start.6 = (f32[1,8,2,8,128]{4,3,2,1,0:T(8,128)S(1)}, f32[1,8,2,8,128]{4,3,2,1,0:T(8,128)S(1)}, u32[]{:S(2)}, u32[]{:S(2)}) collective-permute-start(f32[1,8,2,8,128]{4,3,2,1,0:T(8,128)S(1)} %reshape_reshape.7), channel_id=1, source_target_pairs={{16,0},{32,16},{48,32},{64,48},{80,64},{96,80},{112,96},{0,112},{1... | collective-permute-start | bytes 196616 | tf_op jit(solution)/shard_map/ppermute | solution.py:33
  201.2 4.0 %collective-permute-start.8 = (f32[1,8,1,8,128]{4,3,2,1,0:T(8,128)S(1)}, f32[1,8,1,8,128]{4,3,2,1,0:T(8,128)S(1)}, u32[]{:S(2)}, u32[]{:S(2)}) collective-permute-start(f32[1,8,1,8,128]{4,3,2,1,0:T(8,128)S(1)} %get-tuple-element.177), channel_id=1, source_target_pairs={{4,0},{8,4},{12,8},{0,12},{5,1},{9,5},{13,9},{1,13},{6,2},{10,6},{... | collective-permute-start | bytes 98312 | tf_op jit(solution)/shard_map/ppermute | solution.py:33
  202.0 5.1 %collective-permute-start.9 = (f32[1,8,1,8,128]{4,3,2,1,0:T(8,128)S(1)}, f32[1,8,1,8,128]{4,3,2,1,0:T(8,128)S(1)}, u32[]{:S(2)}, u32[]{:S(2)}) collective-permute-start(f32[1,8,1,8,128]{4,3,2,1,0:T(8,128)S(1)} %get-tuple-element.176), channel_id=1, source_target_pairs={{0,4},{4,8},{8,12},{12,0},{1,5},{5,9},{9,13},{13,1},{2,6},{6,10},{... | collective-permute-start | bytes 98312 | tf_op jit(solution)/shard_map/ppermute | solution.py:32
  203.3 3.9 %collective-permute-start.10 = (f32[1,8,2,1,128]{4,3,2,1,0:T(1,128)S(1)}, f32[1,8,2,1,128]{4,3,2,1,0:T(1,128)S(1)}, u32[]{:S(2)}, u32[]{:S(2)}) collective-permute-start(f32[1,8,2,1,128]{4,3,2,1,0:T(1,128)S(1)} %get-tuple-element.175), channel_id=1, source_target_pairs={{1,0},{2,1},{3,2},{0,3},{5,4},{6,5},{7,6},{4,7},{9,8},{10,9},{11,1... | collective-permute-start | bytes 24584 | tf_op jit(solution)/shard_map/ppermute | solution.py:33
  205.2 3.7 %collective-permute-start.11 = (f32[1,8,2,1,128]{4,3,2,1,0:T(1,128)S(1)}, f32[1,8,2,1,128]{4,3,2,1,0:T(1,128)S(1)}, u32[]{:S(2)}, u32[]{:S(2)}) collective-permute-start(f32[1,8,2,1,128]{4,3,2,1,0:T(1,128)S(1)} %get-tuple-element.174), channel_id=1, source_target_pairs={{0,1},{1,2},{2,3},{3,0},{4,5},{5,6},{6,7},{7,4},{8,9},{9,10},{10,1... | collective-permute-start | bytes 24584 | tf_op jit(solution)/shard_map/ppermute | solution.py:32
where the time goes:
time: 335 us; the launch traced here: 329 us
  matrix products  153 us (46%)
  blocking collectives  92.2 us (28%)
  local copies, waits for them, and re-layouts  59.7 us (18%)
  starting transfers between devices  14.3 us (4%)
  waiting for transfers between devices  6.37 us (2%)
    dot_general x8, matrix products, stacked_product(): jnp.einsum('...kcds,...ksrd->...src', blocks, field, precision=lax.Precis...  153 us
    psum x12, blocking collectives, over_axes(): return functools.reduce(lax.psum, axes, value)  92.2 us
    unnamed x35, local copies, waits for them, and re-layouts  34.5 us
    ppermute x6, starting transfers between devices, extended(): lax.ppermute(initial, axis, [(b, a) for a, b in up])  9.97 us
    slice x1, local copies, waits for them, and re-layouts, apply_operator(): blocks_real = link_blocks[..., 0, :, :, :]  8.86 us
  transfers between devices with their start and end apart: 12, of which 4 were waited for; matrix products, arithmetic and copies ran while one was open for 13% of the time, Pallas kernels for 0%

commit v1 on v0

v1 whole, which is shorter than its diff:
```python
import functools

import jax
import jax.numpy as jnp
from jax import lax
from jax.experimental import pallas as pl
from jax.experimental.pallas import tpu as pltpu
from jax.sharding import PartitionSpec as P

DOF = 32
RHS = 2
SITES = 128
VEC = 128
AXES = ("xy", "gz", "ta")
MESH = pl.DeviceIdType.MESH

mass_shift = 4.0
epsilon = 1e-06

LOCAL = (0, 3, 4)
REMOTE = (1, 2, 5, 6, 7, 8)


def offsets_of(sizes):
    nx, nz, nt = sizes
    first = [(d, 0, 0) for d in range(1, nx)]
    second = [(0, a, b) for a in range(nz) for b in range(nt) if (a, b) != (0, 0)]
    return first, second


def turn(value, shift):
    return pltpu.roll(value, shift % SITES, 1)


def rows_of_sums(tiles, row):
    for half in (4, 2, 1):
        low = (row & half) == 0
        tiles = [
            jnp.where(low, tiles[i], pltpu.roll(tiles[i + half], half, 0))
            + jnp.where(low, pltpu.roll(tiles[i], 8 - half, 0), tiles[i + half])
            for i in range(half)
        ]
    return tiles[0]


def kernel(
    sizes,
    rhs_hbm,
    links_hbm,
    sol_ref,
    res_ref,
    links,
    start,
    field,
    near,
    partial,
    x_in,
    z_out,
    z_in,
    t_out,
    t_in,
    row_out,
    first_in,
    second_in,
    link_sem,
    start_sem,
    halo_send,
    halo_recv,
    first_send,
    first_recv,
    second_send,
    second_recv,
):
    here = [lax.axis_index(name) for name in AXES]
    first, second = offsets_of(sizes)

    def device(offset):
        return tuple(
            here[i] if offset[i] == 0 else lax.rem(here[i] + (offset[i] % sizes[i]), sizes[i])
            for i in range(3)
        )

    barrier = pltpu.get_barrier_semaphore()
    for offset in first + second:
        pl.semaphore_signal(barrier, inc=1, device_id=device(offset), device_id_type=MESH)
    load = pltpu.make_async_copy(rhs_hbm, start, start_sem)
    load.start()
    link_loads = {}
    for k in LOCAL + REMOTE:
        link_loads[k] = pltpu.make_async_copy(links_hbm.at[k], links.at[k], link_sem.at[k])
        link_loads[k].start()

    lane = lax.broadcasted_iota(jnp.int32, (8, SITES), 1)
    row = lax.broadcasted_iota(jnp.int32, (8, SITES), 0)
    lane_z = (lane // 8) % 2
    lane_t = lane % 8

    def wide(mask, rows):
        return jnp.tile(mask, (rows // 8, 1)) if rows > 8 else mask

    def put(k, value):
        for r in range(RHS):
            real = value[64 * r : 64 * r + 32]
            imag = value[64 * r + 32 : 64 * r + 64]
            near[k, r, 0] = real
            near[k, r, 1] = real + imag
            near[k, r, 2] = imag - real

    def remote(j, n, src, dst, offset):
        return pltpu.make_async_remote_copy(
            src_ref=src,
            dst_ref=dst,
            send_sem=halo_send.at[j, n],
            recv_sem=halo_recv.at[j, n],
            device_id=device(offset),
            device_id_type=MESH,
        )

    z_is = [wide(lane_z == p, 64) for p in range(2)]
    t_is = [wide(lane_t == p, 16) for p in range(8)]

    def pack(j, value):
        low, high = value[:64], value[64:]
        z_out[j, 0] = jnp.where(z_is[0], low, turn(high, 8))
        z_out[j, 1] = jnp.where(z_is[1], low, turn(high, -8))
        ahead = value[:16]
        behind = value[112:]
        for g in range(1, 8):
            ahead = jnp.where(t_is[g], turn(value[16 * g : 16 * g + 16], g), ahead)
        for g in range(7):
            behind = jnp.where(t_is[g], turn(value[16 * g : 16 * g + 16], g - 7), behind)
        t_out[j, 0] = ahead
        t_out[j, 1] = behind

    def send(j):
        copies = [
            remote(j, 0, field.at[j], x_in.at[j, 0], (-1, 0, 0)),
            remote(j, 1, field.at[j], x_in.at[j, 1], (1, 0, 0)),
            remote(j, 2, z_out.at[j, 0], z_in.at[j, 0], (0, -1, 0)),
            remote(j, 3, z_out.at[j, 1], z_in.at[j, 1], (0, 1, 0)),
            remote(j, 4, t_out.at[j, 0], t_in.at[j, 0], (0, 0, -1)),
            remote(j, 5, t_out.at[j, 1], t_in.at[j, 1], (0, 0, 1)),
        ]
        for copy in copies:
            copy.start()
        return copies

    def put_local(j):
        value = field[j]
        put(0, value)
        put(3, turn(value, -16))
        put(4, turn(value, 16))

    def put_remote(j):
        put(1, x_in[j, 0])
        put(2, x_in[j, 1])
        value = field[j]
        low, high = value[:64], value[64:]
        came = z_in[j, 0]
        put(
            5,
            jnp.concatenate(
                (
                    jnp.where(z_is[0], turn(low, -8), turn(came, 8)),
                    jnp.where(z_is[0], turn(high, -8), came),
                )
            ),
        )
        came = z_in[j, 1]
        put(
            6,
            jnp.concatenate(
                (
                    jnp.where(z_is[1], turn(low, 8), turn(came, -8)),
                    jnp.where(z_is[1], turn(high, 8), came),
                )
            ),
        )
        came = t_in[j, 0]
        put(
            7,
            jnp.concatenate(
                [
                    jnp.where(t_is[7], turn(came, 7 - g), turn(value[16 * g : 16 * g + 16], -1))
                    for g in range(8)
                ]
            ),
        )
        came = t_in[j, 1]
        put(
            8,
            jnp.concatenate(
                [
                    jnp.where(t_is[0], turn(came, -g), turn(value[16 * g : 16 * g + 16], 1))
                    for g in range(8)
                ]
            ),
        )

    def sweep(ks, target):
        def body(block, carry):
            done = [[] for _ in range(4)]
            for half in range(2):
                sites = [block * 8 + half * 4 + i for i in range(4)]
                if target is None:
                    sums = [[None] * 6 for _ in sites]
                else:
                    sums = [[partial[c, q] for q in range(6)] for c in sites]
                for k in ks:
                    for t in range(4):
                        rows = slice(8 * t, 8 * t + 8)
                        value = [near[k, r, q, rows, :] for r in range(RHS) for q in range(3)]
                        for i, c in enumerate(sites):
                            real = links[k, 0, c, rows, :]
                            imag = links[k, 1, c, rows, :]
                            factors = (real + imag, imag, real)
                            for q in range(6):
                                term = factors[q % 3] * value[q]
                                sums[i][q] = term if sums[i][q] is None else sums[i][q] + term
                for i, c in enumerate(sites):
                    if target is None:
                        for q in range(6):
                            partial[c, q] = sums[i][q]
                    else:
                        for r in range(RHS):
                            done[2 * r].append(sums[i][3 * r] - sums[i][3 * r + 1])
                            done[2 * r + 1].append(sums[i][3 * r] + sums[i][3 * r + 2])
            if target is not None:
                for n in range(4):
                    place = pl.multiple_of(32 * n + block * 8, 8)
                    field[target, pl.ds(place, 8), :] = rows_of_sums(done[n], row)
            return carry

        lax.fori_loop(0, 4, body, 0)

    def parts(j, r):
        return field[j, 64 * r : 64 * r + 32, :], field[j, 64 * r + 32 : 64 * r + 64, :]

    def folded(value):
        value = value[:8] + value[8:16] + value[16:24] + value[24:]
        return jnp.sum(value, axis=1, keepdims=True)

    def gram(pairs, packed):
        for n, i, j, kind in pairs:
            for r in range(RHS):
                ar, ai = parts(i, r)
                br, bi = (ar, ai) if i == j else parts(j, r)
                value = ar * br + ai * bi if kind == 0 else ar * bi - ai * br
                packed = jnp.where(lane == 2 * n + r, folded(value), packed)
        return packed

    load.wait()
    begin = start[...].T
    field[0] = begin
    pack(0, begin)
    pl.semaphore_wait(barrier, len(first) + len(second))
    halos = send(0)
    put_local(0)
    for k in LOCAL:
        link_loads[k].wait()
    sweep(LOCAL, None)
    for k in REMOTE:
        link_loads[k].wait()
    for copy in halos:
        copy.wait_recv()
    put_remote(0)
    sweep(REMOTE, 1)

    again = field[1]
    pack(1, again)
    later = send(1)
    put_local(1)
    sweep(LOCAL, None)
    packed = gram(
        ((0, 0, 0, 0), (1, 0, 1, 0), (2, 0, 1, 1), (3, 1, 1, 0)), jnp.zeros((8, SITES), jnp.float32)
    )
    for copy in later:
        copy.wait_recv()
    put_remote(1)
    sweep(REMOTE, 2)
    packed = gram(
        ((4, 0, 2, 0), (5, 0, 2, 1), (6, 1, 2, 0), (7, 1, 2, 1), (8, 2, 2, 0)), packed
    )

    def reduce_over(offsets, own, index, arrived, send_sem, recv_sem):
        row_out[index] = own
        copies = []
        for n, offset in enumerate(offsets):
            copies.append(
                pltpu.make_async_remote_copy(
                    src_ref=row_out.at[index],
                    dst_ref=arrived.at[n],
                    send_sem=send_sem.at[n],
                    recv_sem=recv_sem.at[n],
                    device_id=device(offset),
                    device_id_type=MESH,
                )
            )
            copies[-1].start()
        total = own
        for n, copy in enumerate(copies):
            copy.wait_recv()
            total = total + arrived[n]
        return total, copies

    own = jnp.sum(packed, axis=0, keepdims=True)
    own, sent_a = reduce_over(first, own, 0, first_in, first_send, first_recv)
    own, sent_b = reduce_over(second, own, 1, second_in, second_send, second_recv)

    spread = jnp.broadcast_to(own, (8, SITES))
    g = [
        jnp.broadcast_to(
            jnp.sum(
                jnp.where((lane == 2 * n + row) & (row < 2), spread, 0.0), axis=1, keepdims=True
            ),
            (8, SITES),
        )
        for n in range(9)
    ]
    g00, g01r, g01i, g11, g02r, g02i, g12r, g12i, g22 = g
    ib = 1.0 / (g00 + epsilon)
    kr = (g01r - mass_shift * epsilon) * ib
    ki = g01i * ib
    hr = kr + mass_shift
    hi = ki
    kk = kr * kr + ki * ki
    wp = (g11 - 2.0 * (kr * g01r + ki * g01i) + kk * g00) * ib
    n1 = wp + epsilon
    in1 = 1.0 / n1
    er = epsilon * hr * ib
    ei = epsilon * hi * ib
    tr = (g02r - (kr * g01r - ki * g01i)) * ib
    ti = (g02i - (kr * g01i + ki * g01r)) * ib
    sr = mass_shift * er + tr
    si = mass_shift * ei + ti
    both = ib * in1
    ur = (g12r - kr * g11 - (kr * g02r + ki * g02i) + kk * g01r) * both
    ui = (g12i - ki * g11 - (kr * g02i - ki * g02r) + kk * g01i) * both
    pr = ur - mass_shift * epsilon * in1
    pi = ui
    h11r = pr + mass_shift
    h11i = pi
    q2 = (g22 - 2.0 * (kr * g12r + ki * g12i) + kk * g11) * both
    cross = sr * (pr * er - pi * ei) + si * (pr * ei + pi * er)
    n2 = (
        q2
        + (sr * sr + si * si) * in1 * (g00 * ib)
        + (pr * pr + pi * pi) * (wp * in1)
        - 2.0 * (sr * tr + si * ti) * in1
        - 2.0 * (pr * ur + pi * ui)
        + 2.0 * cross * in1
        + epsilon
    )
    mr = hr * h11r - hi * h11i - sr
    mi = hr * h11i + hi * h11r - si
    idet = 1.0 / (mr * mr + mi * mi + n2 * (hr * hr + hi * hi + n1))
    x1r = -mr * idet
    x1i = mi * idet
    fr = h11r + kr
    fi = h11i + ki
    x0r = (fr * mr + fi * mi + hr * n2) * idet
    x0i = (fi * mr - fr * mi - hi * n2) * idet

    sol, res = [], []
    for r in range(RHS):
        c0r, c0i, c1r, c1i = (v[r : r + 1, :] for v in (x0r, x0i, x1r, x1i))
        d0r = 1.0 - mass_shift * c0r
        d0i = -mass_shift * c0i
        d1r = mass_shift * c1r + c0r
        d1i = mass_shift * c1i + c0i
        ar, ai = parts(0, r)
        br, bi = parts(1, r)
        cr, ci = parts(2, r)
        sol.append(c0r * ar - c0i * ai + c1r * br - c1i * bi)
        sol.append(c0r * ai + c0i * ar + c1r * bi + c1i * br)
        res.append(d0r * ar - d0i * ai - (d1r * br - d1i * bi) - (c1r * cr - c1i * ci))
        res.append(d0r * ai + d0i * ar - (d1r * bi + d1i * br) - (c1r * ci + c1i * cr))
    sol_ref[...] = jnp.concatenate(sol).T
    res_ref[...] = jnp.concatenate(res).T
    for copy in halos + later + sent_a + sent_b:
        copy.wait_send()


def shards(sizes, right_side, link_blocks):
    first, second = offsets_of(sizes)
    f32 = jnp.float32
    sol, res = pl.pallas_call(
        functools.partial(kernel, sizes),
        out_shape=(
            jax.ShapeDtypeStruct((SITES, VEC), f32),
            jax.ShapeDtypeStruct((SITES, VEC), f32),
        ),
        in_specs=[pl.BlockSpec(memory_space=pl.ANY)] * 2,
        out_specs=(pl.BlockSpec(memory_space=pltpu.VMEM),) * 2,
        scratch_shapes=[
            pltpu.VMEM((9, 2, DOF, DOF, SITES), f32),
            pltpu.VMEM((SITES, VEC), f32),
            pltpu.VMEM((3, VEC, SITES), f32),
            pltpu.VMEM((9, RHS, 3, DOF, SITES), f32),
            pltpu.VMEM((DOF, 6, 8, SITES), f32),
            pltpu.VMEM((2, 2, VEC, SITES), f32),
            pltpu.VMEM((2, 2, 64, SITES), f32),
            pltpu.VMEM((2, 2, 64, SITES), f32),
            pltpu.VMEM((2, 2, 16, SITES), f32),
            pltpu.VMEM((2, 2, 16, SITES), f32),
            pltpu.VMEM((2, 1, SITES), f32),
            pltpu.VMEM((len(first), 1, SITES), f32),
            pltpu.VMEM((len(second), 1, SITES), f32),
            pltpu.SemaphoreType.DMA((9,)),
            pltpu.SemaphoreType.DMA,
            pltpu.SemaphoreType.DMA((2, 6)),
            pltpu.SemaphoreType.DMA((2, 6)),
            pltpu.SemaphoreType.DMA((len(first),)),
            pltpu.SemaphoreType.DMA((len(first),)),
            pltpu.SemaphoreType.DMA((len(second),)),
            pltpu.SemaphoreType.DMA((len(second),)),
        ],
        compiler_params=pltpu.CompilerParams(
            collective_id=0, has_side_effects=True
        ),
    )(
        right_side.reshape(SITES, VEC),
        link_blocks.reshape(9, 2, DOF, DOF, SITES),
    )
    return sol.reshape(right_side.shape), res.reshape(right_side.shape)


def solution(mesh):
    sizes = tuple(mesh.shape[name] for name in AXES)
    spec = P("xy", "gz", "ta", None, None)
    return jax.shard_map(
        functools.partial(shards, sizes),
        mesh=mesh,
        in_specs=(spec, P("xy", "gz", "ta", None, None, None, None, None)),
        out_specs=(spec, spec),
        check_vma=False,
    )
```

time: 335 us -> 32.7 us (0.10)
  the two profiles are of different devices: /device:TPU:2 before, /device:TPU:1 now
where the time goes in v1:
time: 32.7 us; the launch traced here: 32.3 us
  Pallas kernels  28.8 us (88%)
  local copies, waits for them, and re-layouts  2.95 us (9%)
  between operations  0.64 us (2%)
    pallas_call x1, Pallas kernels, shards(): pl.pallas_call(functools.partial(kernel, sizes), out_shape=(jax.ShapeDtyp...  28.8 us
    unnamed x2, local copies, waits for them, and re-layouts  2.95 us

profile of v1, /device:TPU:1, one launch (start us, length us, event | category | flops | bytes accessed | tf_op | source)
XLA Modules:
  0.0 32.3 jit_solution(13966905200546585934)
XLA Ops:
  0.6 28.8 %shard_map.41 = (f32[128,128]{1,0:T(8,128)}, f32[128,128]{1,0:T(8,128)}) custom-call(f32[128,128]{1,0:T(8,128)} %bitcast.5, f32[9,2,32,32,128]{4,3,2,1,0:T(8,128)} %bitcast.4), custom_call_target="tpu_custom_call" | custom-call | tf_op jit(solution)/shard_map/pallas_call | solution.py:387
  29.4 1.5 %copy.6 = f32[1,1,1,128,128]{4,3,2,1,0:T(8,128)} copy(f32[1,1,1,128,128]{4,3,2,1,0:T(8,128)} %bitcast.7) | data formatting | bytes 131072
  30.9 1.5 %copy.7 = f32[1,1,1,128,128]{4,3,2,1,0:T(8,128)} copy(f32[1,1,1,128,128]{4,3,2,1,0:T(8,128)} %bitcast.6) | data formatting | bytes 131072

commit v2 on v1

--- a/solution.py
+++ b/solution.py
@@ -25,7 +25,13 @@
     nx, nz, nt = sizes
     first = [(d, 0, 0) for d in range(1, nx)]
     second = [(0, a, b) for a in range(nz) for b in range(nt) if (a, b) != (0, 0)]
-    return first, second
+
+    def hops(offset):
+        return sum(min(d, n - d) for d, n in zip(offset, sizes))
+
+    beside = [offset for offset in first + second if hops(offset) == 1]
+    further = [offset for offset in first + second if hops(offset) == 2]
+    return first, second, beside, further
 
 
 def turn(value, shift):
@@ -47,8 +53,7 @@
     sizes,
     rhs_hbm,
     links_hbm,
-    sol_ref,
-    res_ref,
+    both_ref,
     links,
     start,
     field,
@@ -70,9 +75,10 @@
     first_recv,
     second_send,
     second_recv,
+    ready,
 ):
     here = [lax.axis_index(name) for name in AXES]
-    first, second = offsets_of(sizes)
+    first, second, beside, further = offsets_of(sizes)
 
     def device(offset):
         return tuple(
@@ -80,11 +86,11 @@
             for i in range(3)
         )
 
-    barrier = pltpu.get_barrier_semaphore()
-    for offset in first + second:
-        pl.semaphore_signal(barrier, inc=1, device_id=device(offset), device_id_type=MESH)
     load = pltpu.make_async_copy(rhs_hbm, start, start_sem)
     load.start()
+    barrier = pltpu.get_barrier_semaphore()
+    for offset in beside:
+        pl.semaphore_signal(barrier, inc=1, device_id=device(offset), device_id_type=MESH)
     link_loads = {}
     for k in LOCAL + REMOTE:
         link_loads[k] = pltpu.make_async_copy(links_hbm.at[k], links.at[k], link_sem.at[k])
@@ -253,7 +259,7 @@
     begin = start[...].T
     field[0] = begin
     pack(0, begin)
-    pl.semaphore_wait(barrier, len(first) + len(second))
+    pl.semaphore_wait(barrier, len(beside))
     halos = send(0)
     put_local(0)
     for k in LOCAL:
@@ -263,6 +269,8 @@
         link_loads[k].wait()
     for copy in halos:
         copy.wait_recv()
+    for offset in further:
+        pl.semaphore_signal(ready, inc=1, device_id=device(offset), device_id_type=MESH)
     put_remote(0)
     sweep(REMOTE, 1)
 
@@ -304,6 +312,7 @@
         return total, copies
 
     own = jnp.sum(packed, axis=0, keepdims=True)
+    pl.semaphore_wait(ready, len(further))
     own, sent_a = reduce_over(first, own, 0, first_in, first_send, first_recv)
     own, sent_b = reduce_over(second, own, 1, second_in, second_send, second_recv)
 
@@ -375,23 +384,25 @@
         sol.append(c0r * ai + c0i * ar + c1r * bi + c1i * br)
         res.append(d0r * ar - d0i * ai - (d1r * br - d1i * bi) - (c1r * cr - c1i * ci))
         res.append(d0r * ai + d0i * ar - (d1r * bi + d1i * br) - (c1r * ci + c1i * cr))
-    sol_ref[...] = jnp.concatenate(sol).T
-    res_ref[...] = jnp.concatenate(res).T
+    both_ref[0] = jnp.concatenate(sol).T
+    both_ref[1] = jnp.concatenate(res).T
     for copy in halos + later + sent_a + sent_b:
         copy.wait_send()
 
 
+def finish(both_ref, sol_ref, res_ref):
+    sol_ref[...] = both_ref[0]
+    res_ref[...] = both_ref[1]
+
+
 def shards(sizes, right_side, link_blocks):
-    first, second = offsets_of(sizes)
+    first, second, _, _ = offsets_of(sizes)
     f32 = jnp.float32
-    sol, res = pl.pallas_call(
+    both = pl.pallas_call(
         functools.partial(kernel, sizes),
-        out_shape=(
-            jax.ShapeDtypeStruct((SITES, VEC), f32),
-            jax.ShapeDtypeStruct((SITES, VEC), f32),
-        ),
+        out_shape=jax.ShapeDtypeStruct((2, SITES, VEC), f32),
         in_specs=[pl.BlockSpec(memory_space=pl.ANY)] * 2,
-        out_specs=(pl.BlockSpec(memory_space=pltpu.VMEM),) * 2,
+        out_specs=pl.BlockSpec(memory_space=pltpu.VMEM),
         scratch_shapes=[
             pltpu.VMEM((9, 2, DOF, DOF, SITES), f32),
             pltpu.VMEM((SITES, VEC), f32),
@@ -414,14 +425,22 @@
             pltpu.SemaphoreType.DMA((len(first),)),
             pltpu.SemaphoreType.DMA((len(second),)),
             pltpu.SemaphoreType.DMA((len(second),)),
+            pltpu.SemaphoreType.REGULAR,
         ],
         compiler_params=pltpu.CompilerParams(
-            collective_id=0, has_side_effects=True
+            collective_id=0, has_side_effects=True, vmem_limit_bytes=54000 * 1024
         ),
     )(
-        right_side.reshape(SITES, VEC),
-        link_blocks.reshape(9, 2, DOF, DOF, SITES),
+        pltpu.with_memory_space_constraint(right_side.reshape(SITES, VEC), pltpu.HBM),
+        pltpu.with_memory_space_constraint(link_blocks.reshape(9, 2, DOF, DOF, SITES), pltpu.HBM),
     )
+    sol, res = pl.pallas_call(
+        finish,
+        out_shape=(jax.ShapeDtypeStruct((SITES, VEC), f32),) * 2,
+        in_specs=[pl.BlockSpec(memory_space=pltpu.VMEM)],
+        out_specs=(pl.BlockSpec(memory_space=pltpu.VMEM),) * 2,
+        compiler_params=pltpu.CompilerParams(vmem_limit_bytes=4 * 1024 * 1024),
+    )(both)
     return sol.reshape(right_side.shape), res.reshape(right_side.shape)
 
 

time: 32.7 us -> 27.5 us (0.84)
  local copies, waits for them, and re-layouts: 2.95 us -> 0 us
  Pallas kernels: 28.8 us -> 26.6 us
    unnamed x2 -> x0, local copies, waits for them, and re-layouts: 2.95 us -> none
    pallas_call x1 -> x2, Pallas kernels: 28.8 us -> 26.6 us  [the longest x1 25.9 us: shards(): pl.pallas_call(functools.partial(kernel, sizes), out_shape=jax.ShapeDtype...]
where the time goes in v2:
time: 27.5 us; the launch traced here: 27.2 us
  Pallas kernels  26.6 us (97%)
  between operations  0.64 us (2%)
    pallas_call x1, Pallas kernels, shards(): pl.pallas_call(functools.partial(kernel, sizes), out_shape=jax.ShapeDtype...  25.9 us
    pallas_call x1, Pallas kernels, shards(): pl.pallas_call(finish, out_shape=(jax.ShapeDtypeStruct((SITES, VEC), f32)...  0.66 us

profile of v2, /device:TPU:1, one launch (start us, length us, event | category | flops | bytes accessed | tf_op | source)
XLA Modules:
  0.0 27.2 jit_solution(17937351604231207439)
XLA Ops:
  0.6 25.9 %shard_map.41.both_ref = f32[2,128,128]{2,1,0:T(8,128)S(1)} custom-call(f32[128,128]{1,0:T(8,128)} %bitcast.5, f32[9,2,32,32,128]{4,3,2,1,0:T(8,128)} %bitcast.4), custom_call_target="tpu_custom_call" | custom-call | tf_op jit(solution)/shard_map/pallas_call | solution.py:401
  26.5 0.7 %shard_map.42 = (f32[128,128]{1,0:T(8,128)}, f32[128,128]{1,0:T(8,128)}) custom-call(f32[2,128,128]{2,1,0:T(8,128)S(1)} %shard_map.41.both_ref), custom_call_target="tpu_custom_call" | custom-call | tf_op jit(solution)/shard_map/pallas_call | solution.py:437

commit v3 on v2

v3 whole, which is shorter than its diff:
```python
import functools

import jax
import jax.numpy as jnp
from jax import lax
from jax.experimental import pallas as pl
from jax.experimental.pallas import tpu as pltpu
from jax.sharding import PartitionSpec as P

DOF = 32
RHS = 2
SITES = 128
VEC = 128
AXES = ("xy", "gz", "ta")
MESH = pl.DeviceIdType.MESH

mass_shift = 4.0
epsilon = 1e-06

LOADS = ((7, 9), (5, 7), (0, 1), (3, 5), (1, 3))
ZOWN, ZFAR, TFAR = 9, 10, 11
OWN_A = (0, 3, 4)
OWN_B = (ZOWN, 7, 8)
FAR = (1, 2, ZFAR, TFAR)


def offsets_of(sizes):
    nx, nz, nt = sizes
    first = [(d, 0, 0) for d in range(1, nx)]
    second = [(0, a, b) for a in range(nz) for b in range(nt) if (a, b) != (0, 0)]

    def hops(offset):
        return sum(min(d, n - d) for d, n in zip(offset, sizes))

    beside = [offset for offset in first + second if hops(offset) == 1]
    further = [offset for offset in first + second if hops(offset) == 2]

    def distance(offset):
        return (min(offset[0], nx - offset[0]) + 1) // 2 + hops((0,) + offset[1:])

    others = [(d, a, b) for d in range(nx) for a in range(nz) for b in range(nt)][1:]
    return first, second, beside, further, sorted(others, key=distance, reverse=True)


def turn(value, shift):
    return pltpu.roll(value, shift % SITES, 1)


def rows_of_sums(tiles, row):
    for half in (4, 2, 1):
        low = (row & half) == 0
        tiles = [
            jnp.where(low, tiles[i], pltpu.roll(tiles[i + half], half, 0))
            + jnp.where(low, pltpu.roll(tiles[i], 8 - half, 0), tiles[i + half])
            for i in range(half)
        ]
    return tiles[0]


def kernel(
    sizes,
    rhs_hbm,
    links_hbm,
    both_ref,
    links,
    start,
    field,
    near,
    partial,
    merged,
    totals,
    folds,
    z_out,
    t_out,
    halo_in,
    row_out,
    arrived,
    link_sem,
    start_sem,
    halo_send,
    halo_recv,
    sum_send,
    sum_recv,
    near_by,
    ready,
    known,
):
    here = [lax.axis_index(name) for name in AXES]
    first, second, beside, further, others = offsets_of(sizes)

    def device(offset):
        return tuple(
            here[i] if offset[i] == 0 else lax.rem(here[i] + (offset[i] % sizes[i]), sizes[i])
            for i in range(3)
        )

    def tell(offsets, semaphore):
        for offset in offsets:
            pl.semaphore_signal(
                semaphore, inc=1, device_id=device(offset), device_id_type=MESH
            )

    load = pltpu.make_async_copy(rhs_hbm, start, start_sem)
    load.start()
    barrier = pltpu.get_barrier_semaphore()
    tell(beside, barrier)
    for n, (begin, end) in enumerate(LOADS):
        for k in range(begin, end):
            pltpu.make_async_copy(links_hbm.at[k], links.at[k], link_sem.at[n]).start()

    def loaded(n):
        whole = links.at[pl.ds(LOADS[n][0], LOADS[n][1] - LOADS[n][0])]
        pltpu.make_async_copy(whole, whole, link_sem.at[n]).wait()

    lane = lax.broadcasted_iota(jnp.int32, (8, SITES), 1)
    row = lax.broadcasted_iota(jnp.int32, (8, SITES), 0)
    lane_z = (lane // 8) % 2
    lane_t = lane % 8

    def wide(mask, rows):
        return jnp.tile(mask, (rows // 8, 1)) if rows > 8 else mask

    def put(k, r, value):
        real = value[:32]
        imag = value[32:]
        near[k, r, 0] = real
        near[k, r, 1] = real + imag
        near[k, r, 2] = imag - real

    def landing(j, r, n):
        return pl.ds(*((0, 64), (64, 64), (128, 32), (160, 32), (192, 8), (200, 8))[n])

    def remote(j, r, n, src, offset):
        return pltpu.make_async_remote_copy(
            src_ref=src,
            dst_ref=halo_in.at[j, r, landing(j, r, n)],
            send_sem=halo_send,
            recv_sem=halo_recv.at[2 * j + r],
            device_id=device(offset),
            device_id_type=MESH,
        )

    def arrive(j, r):
        whole = halo_in.at[j, r]
        pltpu.make_async_copy(whole, whole, halo_recv.at[2 * j + r]).wait()

    z_is = [wide(lane_z == p, 32) for p in range(2)]
    t_is = [lane_t == p for p in range(8)]

    def pack(j, r, value):
        real, imag = value[:32], value[32:]
        z_out[j, r, 0] = jnp.where(z_is[0], real, turn(imag, 8))
        z_out[j, r, 1] = jnp.where(z_is[1], real, turn(imag, -8))
        ahead = value[:8]
        behind = value[56:]
        for g in range(1, 8):
            ahead = jnp.where(t_is[g], turn(value[8 * g : 8 * g + 8], g), ahead)
        for g in range(7):
            behind = jnp.where(t_is[g], turn(value[8 * g : 8 * g + 8], g - 7), behind)
        t_out[j, r, 0] = ahead
        t_out[j, r, 1] = behind

    def send_x(j, r):
        mine = field.at[j, pl.ds(64 * r, 64)]
        remote(j, r, 0, mine, (-1, 0, 0)).start()
        remote(j, r, 1, mine, (1, 0, 0)).start()

    def send_zt(j, r):
        remote(j, r, 2, z_out.at[j, r, 0], (0, -1, 0)).start()
        remote(j, r, 3, z_out.at[j, r, 1], (0, 1, 0)).start()
        remote(j, r, 4, t_out.at[j, r, 0], (0, 0, -1)).start()
        remote(j, r, 5, t_out.at[j, r, 1], (0, 0, 1)).start()

    def put_own(j, r):
        value = field[j, 64 * r : 64 * r + 64, :]
        real, imag = value[:32], value[32:]
        put(0, r, value)
        put(3, r, turn(value, -16))
        put(4, r, turn(value, 16))
        put(
            ZOWN,
            r,
            jnp.concatenate([jnp.where(z_is[0], turn(v, -8), turn(v, 8)) for v in (real, imag)]),
        )
        last, initial = wide(t_is[7], 64), wide(t_is[0], 64)
        put(7, r, jnp.where(last, 0.0, turn(value, -1)))
        put(8, r, jnp.where(initial, 0.0, turn(value, 1)))

    def put_far(j, r):
        put(1, r, halo_in[j, r, 0:64, :])
        put(2, r, halo_in[j, r, 64:128, :])
        ahead, behind = halo_in[j, r, 128:160, :], halo_in[j, r, 160:192, :]
        put(
            ZFAR,
            r,
            jnp.concatenate(
                (
                    jnp.where(z_is[1], turn(ahead, 8), turn(behind, -8)),
                    jnp.where(z_is[1], ahead, behind),
                )
            ),
        )
        ahead, behind = halo_in[j, r, 192:200, :], halo_in[j, r, 200:208, :]
        put(
            TFAR,
            r,
            jnp.concatenate(
                [
                    jnp.where(
                        t_is[7],
                        turn(ahead, 7 - g),
                        jnp.where(t_is[0], turn(behind, -g), 0.0),
                    )
                    for g in range(8)
                ]
            ),
        )

    def coupling(k, part, c, rows):
        return links[k, part, c, rows, :] if k < 9 else merged[k - 9, part, c, rows, :]

    def added(sums, value, real, imag, total):
        factors = (total, imag, real)
        for q in range(len(value)):
            term = factors[q % 3] * value[q]
            sums[q] = term if sums[q] is None else sums[q] + term

    def nearby(k, sides, rows):
        return [near[k, r, q, rows, :] for r in sides for q in range(3)]

    def sweep_own(terms, fresh):
        def body(block, carry):
            for half in range(2):
                sites = [block * 8 + half * 4 + i for i in range(4)]
                sums = [[None if fresh else partial[c, q] for q in range(6)] for c in sites]
                for k in terms:
                    for t in range(4):
                        rows = slice(8 * t, 8 * t + 8)
                        value = nearby(k, range(RHS), rows)
                        for i, c in enumerate(sites):
                            real, imag = coupling(k, 0, c, rows), coupling(k, 1, c, rows)
                            added(sums[i], value, real, imag, real + imag)
                for i, c in enumerate(sites):
                    for q in range(6):
                        partial[c, q] = sums[i][q]
            return carry

        lax.fori_loop(0, 4, body, 0)

    even, last_t = z_is[0][:8], t_is[7]

    def sweep_merging(along_t):
        def body(block, carry):
            for half in range(2):
                sites = [block * 8 + half * 4 + i for i in range(4)]
                if along_t:
                    sums = [[None] * 6 for c in sites]
                else:
                    sums = [[partial[c, q] for q in range(6)] for c in sites]
                for t in range(4):
                    rows = slice(8 * t, 8 * t + 8)
                    terms = (7, 8) if along_t else (ZOWN,)
                    values = [nearby(k, range(RHS), rows) for k in terms]
                    for i, c in enumerate(sites):
                        up, down = (
                            [links[k, part, c, rows, :] for part in range(2)]
                            for k in ((7, 8) if along_t else (5, 6))
                        )
                        if along_t:
                            pairs = (up, down)
                            slot, place = TFAR - 9, 3
                            far = [jnp.where(last_t, a, b) for a, b in zip(up, down)]
                        else:
                            pairs = ([jnp.where(even, a, b) for a, b in zip(up, down)],)
                            slot, place = ZFAR - 9, 2
                            far = [jnp.where(even, b, a) for a, b in zip(up, down)]
                            for part in range(2):
                                merged[ZOWN - 9, part, c, rows, :] = pairs[0][part]
                        for part in range(2):
                            merged[slot, part, c, rows, :] = far[part]
                        totals[place, c, rows, :] = far[0] + far[1]
                        for value, (real, imag) in zip(values, pairs):
                            added(sums[i], value, real, imag, real + imag)
                for i, c in enumerate(sites):
                    for q in range(6):
                        partial[c, q] = sums[i][q]
            return carry

        lax.fori_loop(0, 4, body, 0)

    def total_x():
        def body(block, carry):
            for i in range(4):
                c = block * 4 + i
                for n in range(2):
                    totals[n, c] = links[1 + n, 0, c] + links[1 + n, 1, c]
            return carry

        lax.fori_loop(0, 8, body, 0)

    def sweep_far(j, r):
        def body(block, carry):
            sites = [block * 8 + i for i in range(8)]
            sums = [[partial[c, 3 * r + q] for q in range(3)] for c in sites]
            for n, k in enumerate(FAR):
                for t in range(4):
                    rows = slice(8 * t, 8 * t + 8)
                    value = nearby(k, (r,), rows)
                    for i, c in enumerate(sites):
                        added(
                            sums[i],
                            value,
                            coupling(k, 0, c, rows),
                            coupling(k, 1, c, rows),
                            totals[n, c, rows, :],
                        )
            for i, c in enumerate(sites):
                folds[c, 0] = sums[i][0] - sums[i][1]
                folds[c, 1] = sums[i][0] + sums[i][2]
            return carry

        lax.fori_loop(0, 4, body, 0)
        for part in range(2):
            for block in range(4):
                place = 64 * r + 32 * part + 8 * block
                field[j + 1, place : place + 8, :] = rows_of_sums(
                    [folds[8 * block + i, part] for i in range(8)], row
                )

    def parts(j, r):
        return field[j, 64 * r : 64 * r + 32, :], field[j, 64 * r + 32 : 64 * r + 64, :]

    def folded(value):
        value = value[:8] + value[8:16] + value[16:24] + value[24:]
        return jnp.sum(value, axis=1, keepdims=True)

    def gram(pairs, r, packed):
        for n, i, j, kind in pairs:
            ar, ai = parts(i, r)
            br, bi = (ar, ai) if i == j else parts(j, r)
            value = ar * br + ai * bi if kind == 0 else ar * bi - ai * br
            packed = jnp.where(lane == 2 * n + r, folded(value), packed)
        return packed

    load.wait()
    begin = start[...].T
    field[0] = begin
    for r in range(RHS):
        pack(0, r, begin[64 * r : 64 * r + 64])
    pl.semaphore_wait(barrier, len(beside))
    for r in range(RHS):
        send_x(0, r)
        send_zt(0, r)
    tell(beside, near_by)
    for r in range(RHS):
        put_own(0, r)
    loaded(0)
    sweep_merging(True)
    loaded(1)
    sweep_merging(False)
    loaded(2)
    loaded(3)
    sweep_own(OWN_A, False)
    pl.semaphore_wait(near_by, len(beside))
    tell(further, ready)
    loaded(4)
    total_x()
    for r in range(RHS):
        arrive(0, r)
        put_far(0, r)
        sweep_far(0, r)
        send_x(1, r)
        pack(1, r, field[1, 64 * r : 64 * r + 64, :])
        send_zt(1, r)
    pl.semaphore_wait(ready, len(further))
    tell(second, known)
    for r in range(RHS):
        put_own(1, r)
    sweep_own(OWN_A, True)
    sweep_own(OWN_B, False)
    packed = jnp.zeros((8, SITES), jnp.float32)
    for r in range(RHS):
        packed = gram(((0, 0, 0, 0), (1, 0, 1, 0), (2, 0, 1, 1), (3, 1, 1, 0)), r, packed)
    for r in range(RHS):
        arrive(1, r)
        put_far(1, r)
        sweep_far(1, r)
        packed = gram(
            ((4, 0, 2, 0), (5, 0, 2, 1), (6, 1, 2, 0), (7, 1, 2, 1), (8, 2, 2, 0)), r, packed
        )

    row_out[...] = jnp.sum(packed, axis=0, keepdims=True)
    pl.semaphore_wait(known, len(second))
    for n, offset in enumerate(others):
        pltpu.make_async_remote_copy(
            src_ref=row_out,
            dst_ref=arrived.at[pl.ds(n, 1)],
            send_sem=sum_send,
            recv_sem=sum_recv,
            device_id=device(offset),
            device_id_type=MESH,
        ).start()
    own = row_out[...]
    whole = arrived.at[pl.ds(0, len(others))]
    pltpu.make_async_copy(whole, whole, sum_recv).wait()
    own = own + jnp.sum(arrived[0 : len(others), :], axis=0, keepdims=True)

    spread = jnp.broadcast_to(own, (8, SITES))
    g = [
        jnp.broadcast_to(
            jnp.sum(
                jnp.where((lane == 2 * n + row) & (row < 2), spread, 0.0), axis=1, keepdims=True
            ),
            (8, SITES),
        )
        for n in range(9)
    ]
    g00, g01r, g01i, g11, g02r, g02i, g12r, g12i, g22 = g
    ib = 1.0 / (g00 + epsilon)
    kr = (g01r - mass_shift * epsilon) * ib
    ki = g01i * ib
    hr = kr + mass_shift
    hi = ki
    kk = kr * kr + ki * ki
    wp = (g11 - 2.0 * (kr * g01r + ki * g01i) + kk * g00) * ib
    n1 = wp + epsilon
    in1 = 1.0 / n1
    er = epsilon * hr * ib
    ei = epsilon * hi * ib
    tr = (g02r - (kr * g01r - ki * g01i)) * ib
    ti = (g02i - (kr * g01i + ki * g01r)) * ib
    sr = mass_shift * er + tr
    si = mass_shift * ei + ti
    both = ib * in1
    ur = (g12r - kr * g11 - (kr * g02r + ki * g02i) + kk * g01r) * both
    ui = (g12i - ki * g11 - (kr * g02i - ki * g02r) + kk * g01i) * both
    pr = ur - mass_shift * epsilon * in1
    pi = ui
    h11r = pr + mass_shift
    h11i = pi
    q2 = (g22 - 2.0 * (kr * g12r + ki * g12i) + kk * g11) * both
    cross = sr * (pr * er - pi * ei) + si * (pr * ei + pi * er)
    n2 = (
        q2
        + (sr * sr + si * si) * in1 * (g00 * ib)
        + (pr * pr + pi * pi) * (wp * in1)
        - 2.0 * (sr * tr + si * ti) * in1
        - 2.0 * (pr * ur + pi * ui)
        + 2.0 * cross * in1
        + epsilon
    )
    mr = hr * h11r - hi * h11i - sr
    mi = hr * h11i + hi * h11r - si
    idet = 1.0 / (mr * mr + mi * mi + n2 * (hr * hr + hi * hi + n1))
    x1r = -mr * idet
    x1i = mi * idet
    fr = h11r + kr
    fi = h11i + ki
    x0r = (fr * mr + fi * mi + hr * n2) * idet
    x0i = (fi * mr - fr * mi - hi * n2) * idet

    sol, res = [], []
    for r in range(RHS):
        c0r, c0i, c1r, c1i = (v[r : r + 1, :] for v in (x0r, x0i, x1r, x1i))
        d0r = 1.0 - mass_shift * c0r
        d0i = -mass_shift * c0i
        d1r = mass_shift * c1r + c0r
        d1i = mass_shift * c1i + c0i
        ar, ai = parts(0, r)
        br, bi = parts(1, r)
        cr, ci = parts(2, r)
        sol.append(c0r * ar - c0i * ai + c1r * br - c1i * bi)
        sol.append(c0r * ai + c0i * ar + c1r * bi + c1i * br)
        res.append(d0r * ar - d0i * ai - (d1r * br - d1i * bi) - (c1r * cr - c1i * ci))
        res.append(d0r * ai + d0i * ar - (d1r * bi + d1i * br) - (c1r * ci + c1i * cr))
    both_ref[0] = jnp.concatenate(sol).T
    both_ref[1] = jnp.concatenate(res).T
    pltpu.make_async_copy(halo_in, halo_in, halo_send).wait()
    pltpu.make_async_copy(whole, whole, sum_send).wait()


def finish(both_ref, sol_ref, res_ref):
    sol_ref[...] = both_ref[0]
    res_ref[...] = both_ref[1]


def shards(sizes, right_side, link_blocks):
    others = offsets_of(sizes)[-1]
    f32 = jnp.float32
    both = pl.pallas_call(
        functools.partial(kernel, sizes),
        out_shape=jax.ShapeDtypeStruct((2, SITES, VEC), f32),
        in_specs=[pl.BlockSpec(memory_space=pl.ANY)] * 2,
        out_specs=pl.BlockSpec(memory_space=pltpu.VMEM),
        scratch_shapes=[
            pltpu.VMEM((9, 2, DOF, DOF, SITES), f32),
            pltpu.VMEM((SITES, VEC), f32),
            pltpu.VMEM((3, VEC, SITES), f32),
            pltpu.VMEM((12, RHS, 3, DOF, SITES), f32),
            pltpu.VMEM((DOF, 6, 8, SITES), f32),
            pltpu.VMEM((3, 2, DOF, DOF, SITES), f32),
            pltpu.VMEM((4, DOF, DOF, SITES), f32),
            pltpu.VMEM((DOF, 2, 8, SITES), f32),
            pltpu.VMEM((2, RHS, 2, 32, SITES), f32),
            pltpu.VMEM((2, RHS, 2, 8, SITES), f32),
            pltpu.VMEM((2, RHS, 208, SITES), f32),
            pltpu.VMEM((1, SITES), f32),
            pltpu.VMEM((len(others), SITES), f32),
            pltpu.SemaphoreType.DMA((len(LOADS),)),
            pltpu.SemaphoreType.DMA,
            pltpu.SemaphoreType.DMA,
            pltpu.SemaphoreType.DMA((2 * RHS,)),
            pltpu.SemaphoreType.DMA,
            pltpu.SemaphoreType.DMA,
            pltpu.SemaphoreType.REGULAR,
            pltpu.SemaphoreType.REGULAR,
            pltpu.SemaphoreType.REGULAR,
        ],
        compiler_params=pltpu.CompilerParams(
            collective_id=0, has_side_effects=True, vmem_limit_bytes=54000 * 1024
        ),
    )(
        pltpu.with_memory_space_constraint(right_side.reshape(SITES, VEC), pltpu.HBM),
        pltpu.with_memory_space_constraint(link_blocks.reshape(9, 2, DOF, DOF, SITES), pltpu.HBM),
    )
    sol, res = pl.pallas_call(
        finish,
        out_shape=(jax.ShapeDtypeStruct((SITES, VEC), f32),) * 2,
        in_specs=[pl.BlockSpec(memory_space=pltpu.VMEM)],
        out_specs=(pl.BlockSpec(memory_space=pltpu.VMEM),) * 2,
        compiler_params=pltpu.CompilerParams(vmem_limit_bytes=4 * 1024 * 1024),
    )(both)
    return sol.reshape(right_side.shape), res.reshape(right_side.shape)


def solution(mesh):
    sizes = tuple(mesh.shape[name] for name in AXES)
    spec = P("xy", "gz", "ta", None, None)
    return jax.shard_map(
        functools.partial(shards, sizes),
        mesh=mesh,
        in_specs=(spec, P("xy", "gz", "ta", None, None, None, None, None)),
        out_specs=(spec, spec),
        check_vma=False,
    )
```

time: 27.5 us -> 23.6 us (0.86)
  Pallas kernels: 26.6 us -> 22.9 us
    pallas_call x1, Pallas kernels: 25.9 us -> 22.2 us  [shards(): pl.pallas_call(functools.partial(kernel, sizes), out_shape=jax.ShapeDtype...]
where the time goes in v3:
time: 23.6 us; the launch traced here: 23.5 us
  Pallas kernels  22.9 us (97%)
  between operations  0.64 us (3%)
    pallas_call x1, Pallas kernels, shards(): pl.pallas_call(functools.partial(kernel, sizes), out_shape=jax.ShapeDtype...  22.2 us
    pallas_call x1, Pallas kernels, shards(): pl.pallas_call(finish, out_shape=(jax.ShapeDtypeStruct((SITES, VEC), f32)...  0.66 us

profile of v3, /device:TPU:1, one launch (start us, length us, event | category | flops | bytes accessed | tf_op | source)
XLA Modules:
  0.0 23.5 jit_solution(1626666551744430358)
XLA Ops:
  0.6 22.2 %shard_map.41.both_ref = f32[2,128,128]{2,1,0:T(8,128)S(1)} custom-call(f32[128,128]{1,0:T(8,128)} %bitcast.5, f32[9,2,32,32,128]{4,3,2,1,0:T(8,128)} %bitcast.4), custom_call_target="tpu_custom_call" | custom-call | tf_op jit(solution)/shard_map/pallas_call | solution.py:490
  22.8 0.7 %shard_map.42 = (f32[128,128]{1,0:T(8,128)}, f32[128,128]{1,0:T(8,128)}) custom-call(f32[2,128,128]{2,1,0:T(8,128)S(1)} %shard_map.41.both_ref), custom_call_target="tpu_custom_call" | custom-call | tf_op jit(solution)/shard_map/pallas_call | solution.py:526

commit v4 on v3

--- a/solution.py
+++ b/solution.py
@@ -21,7 +21,9 @@
 ZOWN, ZFAR, TFAR = 9, 10, 11
 OWN_A = (0, 3, 4)
 OWN_B = (ZOWN, 7, 8)
-FAR = (1, 2, ZFAR, TFAR)
+CHIP, OUTER = 1, 2
+FAR = (OUTER, ZFAR, TFAR)
+GROUPS = 2
 
 
 def offsets_of(sizes):
@@ -70,6 +72,7 @@
     merged,
     totals,
     folds,
+    upright,
     z_out,
     t_out,
     halo_in,
@@ -79,6 +82,7 @@
     start_sem,
     halo_send,
     halo_recv,
+    chip_recv,
     sum_send,
     sum_recv,
     near_by,
@@ -102,6 +106,11 @@
 
     load = pltpu.make_async_copy(rhs_hbm, start, start_sem)
     load.start()
+    odd = lax.rem(here[0], 2)
+    partner = (here[0] + 1 - 2 * odd, here[1], here[2])
+    outer = (lax.rem(here[0] + sizes[0] - 1 + 2 * odd, sizes[0]), here[1], here[2])
+    coupling_of = {CHIP: 1 + odd, OUTER: 2 - odd}
+
     barrier = pltpu.get_barrier_semaphore()
     tell(beside, barrier)
     for n, (begin, end) in enumerate(LOADS):
@@ -127,22 +136,24 @@
         near[k, r, 1] = real + imag
         near[k, r, 2] = imag - real
 
-    def landing(j, r, n):
-        return pl.ds(*((0, 64), (64, 64), (128, 32), (160, 32), (192, 8), (200, 8))[n])
-
-    def remote(j, r, n, src, offset):
+    def remote(j, r, place, rows, src, target, arrival):
         return pltpu.make_async_remote_copy(
             src_ref=src,
-            dst_ref=halo_in.at[j, r, landing(j, r, n)],
+            dst_ref=halo_in.at[j, r, pl.ds(place, rows)],
             send_sem=halo_send,
-            recv_sem=halo_recv.at[2 * j + r],
-            device_id=device(offset),
+            recv_sem=arrival.at[2 * j + r],
+            device_id=target,
             device_id_type=MESH,
         )
 
     def arrive(j, r):
-        whole = halo_in.at[j, r]
-        pltpu.make_async_copy(whole, whole, halo_recv.at[2 * j + r]).wait()
+        rest = halo_in.at[j, r, pl.ds(64, 144)]
+        pltpu.make_async_copy(rest, rest, halo_recv.at[2 * j + r]).wait()
+
+    def arrive_chip(j, r):
+        first_rows = halo_in.at[j, r, pl.ds(0, 64)]
+        pltpu.make_async_copy(first_rows, first_rows, chip_recv.at[2 * j + r]).wait()
+        put(CHIP, r, halo_in[j, r, 0:64, :])
 
     z_is = [wide(lane_z == p, 32) for p in range(2)]
     t_is = [lane_t == p for p in range(8)]
@@ -162,14 +173,19 @@
 
     def send_x(j, r):
         mine = field.at[j, pl.ds(64 * r, 64)]
-        remote(j, r, 0, mine, (-1, 0, 0)).start()
-        remote(j, r, 1, mine, (1, 0, 0)).start()
+        remote(j, r, 64, 64, mine, outer, halo_recv).start()
+
+    def send_chip(j, r):
+        mine = field.at[j, pl.ds(64 * r, 64)]
+        remote(j, r, 0, 64, mine, partner, chip_recv).start()
 
     def send_zt(j, r):
-        remote(j, r, 2, z_out.at[j, r, 0], (0, -1, 0)).start()
-        remote(j, r, 3, z_out.at[j, r, 1], (0, 1, 0)).start()
-        remote(j, r, 4, t_out.at[j, r, 0], (0, 0, -1)).start()
-        remote(j, r, 5, t_out.at[j, r, 1], (0, 0, 1)).start()
+        for n in range(2):
+            step = 2 * n - 1
+            target = device((0, step, 0))
+            remote(j, r, 128 + 32 * n, 32, z_out.at[j, r, n], target, halo_recv).start()
+            target = device((0, 0, step))
+            remote(j, r, 192 + 8 * n, 8, t_out.at[j, r, n], target, halo_recv).start()
 
     def put_own(j, r):
         value = field[j, 64 * r : 64 * r + 64, :]
@@ -187,8 +203,7 @@
         put(8, r, jnp.where(initial, 0.0, turn(value, 1)))
 
     def put_far(j, r):
-        put(1, r, halo_in[j, r, 0:64, :])
-        put(2, r, halo_in[j, r, 64:128, :])
+        put(OUTER, r, halo_in[j, r, 64:128, :])
         ahead, behind = halo_in[j, r, 128:160, :], halo_in[j, r, 160:192, :]
         put(
             ZFAR,
@@ -217,7 +232,9 @@
         )
 
     def coupling(k, part, c, rows):
-        return links[k, part, c, rows, :] if k < 9 else merged[k - 9, part, c, rows, :]
+        if k >= 9:
+            return merged[k - 9, part, c, rows, :]
+        return links[coupling_of.get(k, k), part, c, rows, :]
 
     def added(sums, value, real, imag, total):
         factors = (total, imag, real)
@@ -268,11 +285,11 @@
                         )
                         if along_t:
                             pairs = (up, down)
-                            slot, place = TFAR - 9, 3
+                            slot, place = TFAR - 9, 2
                             far = [jnp.where(last_t, a, b) for a, b in zip(up, down)]
                         else:
                             pairs = ([jnp.where(even, a, b) for a, b in zip(up, down)],)
-                            slot, place = ZFAR - 9, 2
+                            slot, place = ZFAR - 9, 1
                             far = [jnp.where(even, b, a) for a, b in zip(up, down)]
                             for part in range(2):
                                 merged[ZOWN - 9, part, c, rows, :] = pairs[0][part]
@@ -288,18 +305,24 @@
 
         lax.fori_loop(0, 4, body, 0)
 
-    def total_x():
+    def total_outer():
         def body(block, carry):
             for i in range(4):
                 c = block * 4 + i
-                for n in range(2):
-                    totals[n, c] = links[1 + n, 0, c] + links[1 + n, 1, c]
+                totals[0, c] = coupling(OUTER, 0, c, slice(None)) + coupling(
+                    OUTER, 1, c, slice(None)
+                )
             return carry
 
         lax.fori_loop(0, 8, body, 0)
 
     def sweep_far(j, r):
-        def body(block, carry):
+        def body(step, carry):
+            for half in range(GROUPS):
+                group(step * GROUPS + half)
+            return carry
+
+        def group(block):
             sites = [block * 8 + i for i in range(8)]
             sums = [[partial[c, 3 * r + q] for q in range(3)] for c in sites]
             for n, k in enumerate(FAR):
@@ -317,9 +340,8 @@
             for i, c in enumerate(sites):
                 folds[c, 0] = sums[i][0] - sums[i][1]
                 folds[c, 1] = sums[i][0] + sums[i][2]
-            return carry
-
-        lax.fori_loop(0, 4, body, 0)
+
+        lax.fori_loop(0, 4 // GROUPS, body, 0)
         for part in range(2):
             for block in range(4):
                 place = 64 * r + 32 * part + 8 * block
@@ -351,6 +373,8 @@
     for r in range(RHS):
         send_x(0, r)
         send_zt(0, r)
+    for r in range(RHS):
+        send_chip(0, r)
     tell(beside, near_by)
     for r in range(RHS):
         put_own(0, r)
@@ -364,7 +388,10 @@
     pl.semaphore_wait(near_by, len(beside))
     tell(further, ready)
     loaded(4)
-    total_x()
+    total_outer()
+    for r in range(RHS):
+        arrive_chip(0, r)
+    sweep_own((CHIP,), False)
     for r in range(RHS):
         arrive(0, r)
         put_far(0, r)
@@ -372,12 +399,16 @@
         send_x(1, r)
         pack(1, r, field[1, 64 * r : 64 * r + 64, :])
         send_zt(1, r)
+        send_chip(1, r)
     pl.semaphore_wait(ready, len(further))
     tell(second, known)
     for r in range(RHS):
         put_own(1, r)
     sweep_own(OWN_A, True)
     sweep_own(OWN_B, False)
+    for r in range(RHS):
+        arrive_chip(1, r)
+    sweep_own((CHIP,), False)
     packed = jnp.zeros((8, SITES), jnp.float32)
     for r in range(RHS):
         packed = gram(((0, 0, 0, 0), (1, 0, 1, 0), (2, 0, 1, 1), (3, 1, 1, 0)), r, packed)
@@ -385,6 +416,7 @@
         arrive(1, r)
         put_far(1, r)
         sweep_far(1, r)
+    for r in range(RHS):
         packed = gram(
             ((4, 0, 2, 0), (5, 0, 2, 1), (6, 1, 2, 0), (7, 1, 2, 1), (8, 2, 2, 0)), r, packed
         )
@@ -400,21 +432,28 @@
             device_id=device(offset),
             device_id_type=MESH,
         ).start()
+    is_real = (lax.broadcasted_iota(jnp.int32, (SITES, VEC), 1) // 32) % 2 == 0
+
+    def rotated(value):
+        return jnp.where(is_real, -turn(value, -32), turn(value, 32))
+
+    upright[0] = rotated(start[...])
+    for j in (1, 2):
+        value = field[j].T
+        upright[2 * j - 1] = value
+        upright[2 * j] = rotated(value)
     own = row_out[...]
     whole = arrived.at[pl.ds(0, len(others))]
     pltpu.make_async_copy(whole, whole, sum_recv).wait()
     own = own + jnp.sum(arrived[0 : len(others), :], axis=0, keepdims=True)
 
     spread = jnp.broadcast_to(own, (8, SITES))
-    g = [
-        jnp.broadcast_to(
-            jnp.sum(
-                jnp.where((lane == 2 * n + row) & (row < 2), spread, 0.0), axis=1, keepdims=True
-            ),
-            (8, SITES),
-        )
-        for n in range(9)
-    ]
+
+    def total(n, r):
+        chosen = jnp.where(lane == 2 * n + r, spread, 0.0)
+        return jnp.broadcast_to(jnp.sum(chosen, axis=1, keepdims=True), (8, SITES))
+
+    g = [jnp.where(lane < 64, total(n, 0), total(n, 1)) for n in range(9)]
     g00, g01r, g01i, g11, g02r, g02i, g12r, g12i, g22 = g
     ib = 1.0 / (g00 + epsilon)
     kr = (g01r - mass_shift * epsilon) * ib
@@ -459,29 +498,31 @@
     x0r = (fr * mr + fi * mi + hr * n2) * idet
     x0i = (fi * mr - fr * mi - hi * n2) * idet
 
-    sol, res = [], []
-    for r in range(RHS):
-        c0r, c0i, c1r, c1i = (v[r : r + 1, :] for v in (x0r, x0i, x1r, x1i))
-        d0r = 1.0 - mass_shift * c0r
-        d0i = -mass_shift * c0i
-        d1r = mass_shift * c1r + c0r
-        d1i = mass_shift * c1i + c0i
-        ar, ai = parts(0, r)
-        br, bi = parts(1, r)
-        cr, ci = parts(2, r)
-        sol.append(c0r * ar - c0i * ai + c1r * br - c1i * bi)
-        sol.append(c0r * ai + c0i * ar + c1r * bi + c1i * br)
-        res.append(d0r * ar - d0i * ai - (d1r * br - d1i * bi) - (c1r * cr - c1i * ci))
-        res.append(d0r * ai + d0i * ar - (d1r * bi + d1i * br) - (c1r * ci + c1i * cr))
-    both_ref[0] = jnp.concatenate(sol).T
-    both_ref[1] = jnp.concatenate(res).T
+    d0r = 1.0 - mass_shift * x0r
+    d0i = -mass_shift * x0i
+    d1r = mass_shift * x1r + x0r
+    d1i = mass_shift * x1i + x0i
+    for n in range(SITES // 8):
+        rows = slice(8 * n, 8 * n + 8)
+        a, ia = start[rows, :], upright[0, rows, :]
+        b, ib_, c, ic = (upright[k, rows, :] for k in range(1, 5))
+        both_ref[0, rows, :] = x0r * a + x0i * ia + x1r * b + x1i * ib_
+        both_ref[1, rows, :] = (
+            d0r * a + d0i * ia - (d1r * b + d1i * ib_) - (x1r * c + x1i * ic)
+        )
     pltpu.make_async_copy(halo_in, halo_in, halo_send).wait()
     pltpu.make_async_copy(whole, whole, sum_send).wait()
 
 
-def finish(both_ref, sol_ref, res_ref):
-    sol_ref[...] = both_ref[0]
-    res_ref[...] = both_ref[1]
+def finish(both_ref, sol_ref, res_ref, sems):
+    copies = [
+        pltpu.make_async_copy(both_ref.at[n], out, sems.at[n])
+        for n, out in enumerate((sol_ref, res_ref))
+    ]
+    for copy in copies:
+        copy.start()
+    for copy in copies:
+        copy.wait()
 
 
 def shards(sizes, right_side, link_blocks):
@@ -499,8 +540,9 @@
             pltpu.VMEM((12, RHS, 3, DOF, SITES), f32),
             pltpu.VMEM((DOF, 6, 8, SITES), f32),
             pltpu.VMEM((3, 2, DOF, DOF, SITES), f32),
-            pltpu.VMEM((4, DOF, DOF, SITES), f32),
+            pltpu.VMEM((3, DOF, DOF, SITES), f32),
             pltpu.VMEM((DOF, 2, 8, SITES), f32),
+            pltpu.VMEM((5, SITES, VEC), f32),
             pltpu.VMEM((2, RHS, 2, 32, SITES), f32),
             pltpu.VMEM((2, RHS, 2, 8, SITES), f32),
             pltpu.VMEM((2, RHS, 208, SITES), f32),
@@ -509,6 +551,7 @@
             pltpu.SemaphoreType.DMA((len(LOADS),)),
             pltpu.SemaphoreType.DMA,
             pltpu.SemaphoreType.DMA,
+            pltpu.SemaphoreType.DMA((2 * RHS,)),
             pltpu.SemaphoreType.DMA((2 * RHS,)),
             pltpu.SemaphoreType.DMA,
             pltpu.SemaphoreType.DMA,
@@ -527,7 +570,8 @@
         finish,
         out_shape=(jax.ShapeDtypeStruct((SITES, VEC), f32),) * 2,
         in_specs=[pl.BlockSpec(memory_space=pltpu.VMEM)],
-        out_specs=(pl.BlockSpec(memory_space=pltpu.VMEM),) * 2,
+        out_specs=(pl.BlockSpec(memory_space=pl.ANY),) * 2,
+        scratch_shapes=[pltpu.SemaphoreType.DMA((2,))],
         compiler_params=pltpu.CompilerParams(vmem_limit_bytes=4 * 1024 * 1024),
     )(both)
     return sol.reshape(right_side.shape), res.reshape(right_side.shape)

time: 23.6 us -> 23.1 us (0.979)
  Pallas kernels: 22.9 us -> 22.3 us
    pallas_call x1, Pallas kernels: 22.2 us -> 21.7 us  [shards(): pl.pallas_call(functools.partial(kernel, sizes), out_shape=jax.ShapeDtype...]
where the time goes in v4:
time: 23.1 us; the launch traced here: 23 us
  Pallas kernels  22.3 us (97%)
  between operations  0.64 us (3%)
    pallas_call x1, Pallas kernels, shards(): pl.pallas_call(functools.partial(kernel, sizes), out_shape=jax.ShapeDtype...  21.7 us
    pallas_call x1, Pallas kernels, shards(): pl.pallas_call(finish, out_shape=(jax.ShapeDtypeStruct((SITES, VEC), f32)...  0.67 us

profile of v4, /device:TPU:1, one launch (start us, length us, event | category | flops | bytes accessed | tf_op | source)
XLA Modules:
  0.0 23.0 jit_solution(4649848387949709422)
XLA Ops:
  0.6 21.7 %shard_map.41.both_ref = f32[2,128,128]{2,1,0:T(8,128)S(1)} custom-call(f32[128,128]{1,0:T(8,128)} %bitcast.5, f32[9,2,32,32,128]{4,3,2,1,0:T(8,128)} %bitcast.4), custom_call_target="tpu_custom_call" | custom-call | tf_op jit(solution)/shard_map/pallas_call | solution.py:531
  22.3 0.7 %shard_map.42 = (f32[128,128]{1,0:T(8,128)}, f32[128,128]{1,0:T(8,128)}) custom-call(f32[2,128,128]{2,1,0:T(8,128)S(1)} %shard_map.41.both_ref), custom_call_target="tpu_custom_call" | custom-call | tf_op jit(solution)/shard_map/pallas_call | solution.py:569

commit v5 on v4

--- a/solution.py
+++ b/solution.py
@@ -23,7 +23,6 @@
 OWN_B = (ZOWN, 7, 8)
 CHIP, OUTER = 1, 2
 FAR = (OUTER, ZFAR, TFAR)
-GROUPS = 2
 
 
 def offsets_of(sizes):
@@ -71,7 +70,6 @@
     partial,
     merged,
     totals,
-    folds,
     upright,
     z_out,
     t_out,
@@ -83,6 +81,7 @@
     halo_send,
     halo_recv,
     chip_recv,
+    outer_recv,
     sum_send,
     sum_recv,
     near_by,
@@ -147,8 +146,13 @@
         )
 
     def arrive(j, r):
-        rest = halo_in.at[j, r, pl.ds(64, 144)]
+        rest = halo_in.at[j, r, pl.ds(128, 80)]
         pltpu.make_async_copy(rest, rest, halo_recv.at[2 * j + r]).wait()
+
+    def arrive_outer(j, r):
+        rest = halo_in.at[j, r, pl.ds(64, 64)]
+        pltpu.make_async_copy(rest, rest, outer_recv.at[2 * j + r]).wait()
+        put(OUTER, r, halo_in[j, r, 64:128, :])
 
     def arrive_chip(j, r):
         first_rows = halo_in.at[j, r, pl.ds(0, 64)]
@@ -173,7 +177,7 @@
 
     def send_x(j, r):
         mine = field.at[j, pl.ds(64 * r, 64)]
-        remote(j, r, 64, 64, mine, outer, halo_recv).start()
+        remote(j, r, 64, 64, mine, outer, outer_recv).start()
 
     def send_chip(j, r):
         mine = field.at[j, pl.ds(64 * r, 64)]
@@ -203,7 +207,6 @@
         put(8, r, jnp.where(initial, 0.0, turn(value, 1)))
 
     def put_far(j, r):
-        put(OUTER, r, halo_in[j, r, 64:128, :])
         ahead, behind = halo_in[j, r, 128:160, :], halo_in[j, r, 160:192, :]
         put(
             ZFAR,
@@ -316,38 +319,60 @@
 
         lax.fori_loop(0, 8, body, 0)
 
-    def sweep_far(j, r):
+    def sweep_far(r, terms):
         def body(step, carry):
-            for half in range(GROUPS):
-                group(step * GROUPS + half)
+            for half in range(2):
+                sites = [step * 16 + half * 8 + i for i in range(8)]
+                sums = [[partial[c, 3 * r + q] for q in range(3)] for c in sites]
+                for k in terms:
+                    for t in range(4):
+                        rows = slice(8 * t, 8 * t + 8)
+                        value = nearby(k, (r,), rows)
+                        for i, c in enumerate(sites):
+                            added(
+                                sums[i],
+                                value,
+                                coupling(k, 0, c, rows),
+                                coupling(k, 1, c, rows),
+                                totals[FAR.index(k), c, rows, :],
+                            )
+                for i, c in enumerate(sites):
+                    for q in range(3):
+                        partial[c, 3 * r + q] = sums[i][q]
             return carry
 
-        def group(block):
-            sites = [block * 8 + i for i in range(8)]
-            sums = [[partial[c, 3 * r + q] for q in range(3)] for c in sites]
-            for n, k in enumerate(FAR):
-                for t in range(4):
-                    rows = slice(8 * t, 8 * t + 8)
-                    value = nearby(k, (r,), rows)
-                    for i, c in enumerate(sites):
-                        added(
-                            sums[i],
-                            value,
-                            coupling(k, 0, c, rows),
-                            coupling(k, 1, c, rows),
-                            totals[n, c, rows, :],
-                        )
-            for i, c in enumerate(sites):
-                folds[c, 0] = sums[i][0] - sums[i][1]
-                folds[c, 1] = sums[i][0] + sums[i][2]
-
-        lax.fori_loop(0, 4 // GROUPS, body, 0)
-        for part in range(2):
-            for block in range(4):
-                place = 64 * r + 32 * part + 8 * block
-                field[j + 1, place : place + 8, :] = rows_of_sums(
-                    [folds[8 * block + i, part] for i in range(8)], row
-                )
+        lax.fori_loop(0, 2, body, 0)
+
+    def finish_far(j, r):
+        for block in range(4):
+            sums = [[partial[8 * block + i, 3 * r + q] for q in range(3)] for i in range(8)]
+            place = 64 * r + 8 * block
+            field[j + 1, place : place + 8, :] = rows_of_sums([a - b for a, b, _ in sums], row)
+            field[j + 1, place + 32 : place + 40, :] = rows_of_sums(
+                [a + b for a, _, b in sums], row
+            )
+
+    def from_outer(j, r):
+        arrive_outer(j, r)
+        sweep_far(r, (OUTER,))
+
+    def from_zt(j, r):
+        arrive(j, r)
+        put_far(j, r)
+        sweep_far(r, (ZFAR, TFAR))
+
+    def far_terms(j, r):
+        @pl.when(odd == 0)
+        def _():
+            from_outer(j, r)
+            from_zt(j, r)
+
+        @pl.when(odd == 1)
+        def _():
+            from_zt(j, r)
+            from_outer(j, r)
+
+        finish_far(j, r)
 
     def parts(j, r):
         return field[j, 64 * r : 64 * r + 32, :], field[j, 64 * r + 32 : 64 * r + 64, :]
@@ -393,9 +418,7 @@
         arrive_chip(0, r)
     sweep_own((CHIP,), False)
     for r in range(RHS):
-        arrive(0, r)
-        put_far(0, r)
-        sweep_far(0, r)
+        far_terms(0, r)
         send_x(1, r)
         pack(1, r, field[1, 64 * r : 64 * r + 64, :])
         send_zt(1, r)
@@ -413,9 +436,7 @@
     for r in range(RHS):
         packed = gram(((0, 0, 0, 0), (1, 0, 1, 0), (2, 0, 1, 1), (3, 1, 1, 0)), r, packed)
     for r in range(RHS):
-        arrive(1, r)
-        put_far(1, r)
-        sweep_far(1, r)
+        far_terms(1, r)
     for r in range(RHS):
         packed = gram(
             ((4, 0, 2, 0), (5, 0, 2, 1), (6, 1, 2, 0), (7, 1, 2, 1), (8, 2, 2, 0)), r, packed
@@ -541,7 +562,6 @@
             pltpu.VMEM((DOF, 6, 8, SITES), f32),
             pltpu.VMEM((3, 2, DOF, DOF, SITES), f32),
             pltpu.VMEM((3, DOF, DOF, SITES), f32),
-            pltpu.VMEM((DOF, 2, 8, SITES), f32),
             pltpu.VMEM((5, SITES, VEC), f32),
             pltpu.VMEM((2, RHS, 2, 32, SITES), f32),
             pltpu.VMEM((2, RHS, 2, 8, SITES), f32),
@@ -551,6 +571,7 @@
             pltpu.SemaphoreType.DMA((len(LOADS),)),
             pltpu.SemaphoreType.DMA,
             pltpu.SemaphoreType.DMA,
+            pltpu.SemaphoreType.DMA((2 * RHS,)),
             pltpu.SemaphoreType.DMA((2 * RHS,)),
             pltpu.SemaphoreType.DMA((2 * RHS,)),
             pltpu.SemaphoreType.DMA,

time: 23.1 us -> 22.9 us (level)
  no operation moved by 1% of the time
where the time goes in v5:
time: 22.9 us; the launch traced here: 22.8 us
  Pallas kernels  22.2 us (97%)
  between operations  0.64 us (3%)
    pallas_call x1, Pallas kernels, shards(): pl.pallas_call(functools.partial(kernel, sizes), out_shape=jax.ShapeDtype...  21.5 us
    pallas_call x1, Pallas kernels, shards(): pl.pallas_call(finish, out_shape=(jax.ShapeDtypeStruct((SITES, VEC), f32)...  0.67 us

profile of v5, /device:TPU:1, one launch (start us, length us, event | category | flops | bytes accessed | tf_op | source)
XLA Modules:
  0.0 22.8 jit_solution(11144002837915500558)
XLA Ops:
  0.6 21.5 %shard_map.41.both_ref = f32[2,128,128]{2,1,0:T(8,128)S(1)} custom-call(f32[128,128]{1,0:T(8,128)} %bitcast.5, f32[9,2,32,32,128]{4,3,2,1,0:T(8,128)} %bitcast.4), custom_call_target="tpu_custom_call" | custom-call | tf_op jit(solution)/shard_map/pallas_call | solution.py:552
  22.1 0.7 %shard_map.42 = (f32[128,128]{1,0:T(8,128)}, f32[128,128]{1,0:T(8,128)}) custom-call(f32[2,128,128]{2,1,0:T(8,128)S(1)} %shard_map.41.both_ref), custom_call_target="tpu_custom_call" | custom-call | tf_op jit(solution)/shard_map/pallas_call | solution.py:590

commit v6 on v5

--- a/solution.py
+++ b/solution.py
@@ -17,7 +17,7 @@
 mass_shift = 4.0
 epsilon = 1e-06
 
-LOADS = ((7, 9), (5, 7), (0, 1), (3, 5), (1, 3))
+LOADS = ((0, 1), (7, 9), (5, 7), (3, 5), (1, 3))
 ZOWN, ZFAR, TFAR = 9, 10, 11
 OWN_A = (0, 3, 4)
 OWN_B = (ZOWN, 7, 8)
@@ -183,13 +183,20 @@
         mine = field.at[j, pl.ds(64 * r, 64)]
         remote(j, r, 0, 64, mine, partner, chip_recv).start()
 
-    def send_zt(j, r):
+    def send_t(j, r):
         for n in range(2):
-            step = 2 * n - 1
-            target = device((0, step, 0))
-            remote(j, r, 128 + 32 * n, 32, z_out.at[j, r, n], target, halo_recv).start()
-            target = device((0, 0, step))
+            target = device((0, 0, 2 * n - 1))
             remote(j, r, 192 + 8 * n, 8, t_out.at[j, r, n], target, halo_recv).start()
+
+    def send_z(j, sides, core):
+        @pl.when(odd == core)
+        def _():
+            for r in sides:
+                for n in range(2):
+                    target = device((0, 2 * n - 1, 0))
+                    remote(
+                        j, r, 128 + 32 * n, 32, z_out.at[j, r, n], target, halo_recv
+                    ).start()
 
     def put_own(j, r):
         value = field[j, 64 * r : 64 * r + 64, :]
@@ -273,10 +280,7 @@
         def body(block, carry):
             for half in range(2):
                 sites = [block * 8 + half * 4 + i for i in range(4)]
-                if along_t:
-                    sums = [[None] * 6 for c in sites]
-                else:
-                    sums = [[partial[c, q] for q in range(6)] for c in sites]
+                sums = [[partial[c, q] for q in range(6)] for c in sites]
                 for t in range(4):
                     rows = slice(8 * t, 8 * t + 8)
                     terms = (7, 8) if along_t else (ZOWN,)
@@ -396,20 +400,23 @@
         pack(0, r, begin[64 * r : 64 * r + 64])
     pl.semaphore_wait(barrier, len(beside))
     for r in range(RHS):
+        send_z(0, (r,), 0)
         send_x(0, r)
-        send_zt(0, r)
+        send_t(0, r)
     for r in range(RHS):
         send_chip(0, r)
     tell(beside, near_by)
     for r in range(RHS):
         put_own(0, r)
+    send_z(0, range(RHS), 1)
     loaded(0)
+    sweep_own((0,), True)
+    loaded(1)
     sweep_merging(True)
-    loaded(1)
+    loaded(2)
     sweep_merging(False)
-    loaded(2)
     loaded(3)
-    sweep_own(OWN_A, False)
+    sweep_own((3, 4), False)
     pl.semaphore_wait(near_by, len(beside))
     tell(further, ready)
     loaded(4)
@@ -421,12 +428,14 @@
         far_terms(0, r)
         send_x(1, r)
         pack(1, r, field[1, 64 * r : 64 * r + 64, :])
-        send_zt(1, r)
+        send_z(1, (r,), 0)
+        send_t(1, r)
         send_chip(1, r)
     pl.semaphore_wait(ready, len(further))
     tell(second, known)
     for r in range(RHS):
         put_own(1, r)
+    send_z(1, range(RHS), 1)
     sweep_own(OWN_A, True)
     sweep_own(OWN_B, False)
     for r in range(RHS):

time: 22.9 us -> 22.9 us (level)
  no operation moved by 1% of the time
where the time goes in v6:
time: 22.9 us; the launch traced here: 22.8 us
  Pallas kernels  22.2 us (97%)
  between operations  0.64 us (3%)
    pallas_call x1, Pallas kernels, shards(): pl.pallas_call(functools.partial(kernel, sizes), out_shape=jax.ShapeDtype...  21.5 us
    pallas_call x1, Pallas kernels, shards(): pl.pallas_call(finish, out_shape=(jax.ShapeDtypeStruct((SITES, VEC), f32)...  0.67 us

profile of v6, /device:TPU:1, one launch (start us, length us, event | category | flops | bytes accessed | tf_op | source)
XLA Modules:
  0.0 22.8 jit_solution(14149513012405928522)
XLA Ops:
  0.6 21.5 %shard_map.41.both_ref = f32[2,128,128]{2,1,0:T(8,128)S(1)} custom-call(f32[128,128]{1,0:T(8,128)} %bitcast.5, f32[9,2,32,32,128]{4,3,2,1,0:T(8,128)} %bitcast.4), custom_call_target="tpu_custom_call" | custom-call | tf_op jit(solution)/shard_map/pallas_call | solution.py:561
  22.2 0.7 %shard_map.42 = (f32[128,128]{1,0:T(8,128)}, f32[128,128]{1,0:T(8,128)}) custom-call(f32[2,128,128]{2,1,0:T(8,128)S(1)} %shard_map.41.both_ref), custom_call_target="tpu_custom_call" | custom-call | tf_op jit(solution)/shard_map/pallas_call | solution.py:599
